TPU v7x, 256 devices: a whole 4x4x8 slice. The times are simulated.
256 devices in a mesh: curve: 64 (over y, z, core), sub: 4 (over x).
Axes of the slice: x: 4, y: 4, z: 8, core: 2. Of those that a mesh axis runs over, the one named last changes fastest.
Arguments:
- forcing: float32 [12, 6144, 1024], P(None, 'curve', 'sub'), may hold values from -10 to 10
- metric: float32 [6144, 1024], P('curve', 'sub'), may hold values from 0.25 to 4
- jacobian: float32 [6144, 1024], P('curve', 'sub'), may hold values from 0.5 to 2
- mode_scale: float32 [12], replicated, may hold values from 0.1 to 10
Outputs:
- solution: float32 [12, 6144, 1024], P(None, 'curve', 'sub')
- residual: float32 [12, 6144, 1024], P(None, 'curve', 'sub')
All inputs are finite; a program needn't handle non-finite values.
Results may differ from a plain program's by a relative error of at most 0.0003.
Values sent between devices are 32-bit elements; how exact they have to be, the bound alone decides.
A program may use at most 64 MiB of HBM per device.

v0:
```python
import functools
import math

import jax
import jax.numpy as jnp
import numpy as np
from jax import lax
from jax.experimental import pallas as pl
from jax.experimental.pallas import tpu as pltpu
from jax.sharding import PartitionSpec as P

ITERS = 3
GROUPS = 2
UNROLL = True
MESH = pl.DeviceIdType.MESH
LANES = 128
f32 = jnp.float32
bf16 = jnp.bfloat16


def gll_tables():
    points = np.array([-1.0, -1.0 / math.sqrt(5.0), 1.0 / math.sqrt(5.0), 1.0])
    weights = np.array([1.0 / 6.0, 5.0 / 6.0, 5.0 / 6.0, 1.0 / 6.0])
    factor = np.array(
        [np.prod([points[j] - points[m] for m in range(4) if m != j]) for j in range(4)]
    )
    slopes = np.zeros((4, 4))
    for i in range(4):
        for j in range(4):
            if i != j:
                slopes[i, j] = factor[i] / (factor[j] * (points[i] - points[j]))
        slopes[i, i] = sum((1.0 / (points[i] - points[m]) for m in range(4) if m != i))
    return (slopes, weights)


SLOPES, WEIGHTS = gll_tables()


def combo(coefs, parts):
    total = None
    for c, v in zip(coefs, parts):
        if abs(c) < 1e-12:
            continue
        term = v * f32(c)
        total = term if total is None else total + term
    return total


def kernel(
    nc, ns, modes, groups,
    scale_hbm, forcing_ref, metric_ref, jac_ref, grad_hbm, div_hbm,
    x, r,
    z, d, s, w, invp, mass, flux, zcat, gout, sums, coef,
    row_tx, row_rx, col_tx, col_rx, cor_rx, ar_tx, ar_rx,
    source, factors, grad_ref, div_ref, scale_ref,
    htx_sem, hrx_sem, atx_sem, arx_sem, in_sem, table_sem,
):
    rows, cols = metric_ref.shape
    q = rows // 4
    n = nc * ns
    half = cols - LANES
    tiles = cols // LANES
    per = modes // groups
    slots = row_tx.shape[2]
    loads, sources = [], []
    for c in range(tiles):
        cut = pl.ds(c * LANES, LANES)
        loads += [
            pltpu.make_async_copy(jac_ref.at[:, cut], factors.at[0, c], in_sem.at[0, c]),
            pltpu.make_async_copy(metric_ref.at[:, cut], factors.at[1, c], in_sem.at[1, c]),
        ]
        sources.append(
            pltpu.make_async_copy(forcing_ref.at[:, :, cut], source.at[c], in_sem.at[2, c]))
    div_load = pltpu.make_async_copy(div_hbm, div_ref, table_sem.at[0])
    grad_load = pltpu.make_async_copy(grad_hbm, grad_ref, table_sem.at[1])
    scale_load = pltpu.make_async_copy(scale_hbm, scale_ref, table_sem.at[2])
    for copy in loads + sources + [div_load, scale_load, grad_load]:
        copy.start()

    me_c, me_s = lax.axis_index("curve"), lax.axis_index("sub")
    me = me_c * ns + me_s
    up, down = lax.rem(me_c + nc - 1, nc), lax.rem(me_c + 1, nc)
    left, right = lax.rem(me_s + ns - 1, ns), lax.rem(me_s + 1, ns)

    def place(offset):
        target = lax.rem(me + offset, n)
        return (target // ns, lax.rem(target, ns))

    barrier = pltpu.get_barrier_semaphore()

    def greet(offset, carry):
        pl.semaphore_signal(barrier, inc=1, device_id=place(offset), device_id_type=MESH)
        return carry

    lax.fori_loop(1, n, greet, 0)

    lane_full = lax.broadcasted_iota(jnp.int32, (q, cols), 1)
    lane = lax.broadcasted_iota(jnp.int32, (q, LANES), 1)
    row_at = lax.broadcasted_iota(jnp.int32, (q, cols), 0)
    phase = lane_full % 4
    on_edge = (phase == 0) | (phase == 3)
    take_next = (phase == 3) & (lane_full != cols - 1)
    take_prev = (phase == 0) & (lane_full != 0)

    def load(ref, m):
        return [ref[m, p * q:(p + 1) * q, :] for p in range(4)]

    def save(ref, m, parts):
        for p in range(4):
            ref[m, p * q:(p + 1) * q, :] = parts[p]

    def load2(ref):
        return [ref[p * q:(p + 1) * q, :] for p in range(4)]

    def pack(k, m, slot, h, tops):
        lo, hi = tops
        row_tx[k, 0, pl.ds(slot, 1), :] = h[0][0:1, :]
        row_tx[k, 1, pl.ds(slot, 1), :] = h[3][q - 1:q, :]
        t0 = h[0] + jnp.where(row_at == 0, 0.0, pltpu.roll(h[3], 1, 0))
        t3 = h[3] + jnp.where(row_at == q - 1, 0.0, pltpu.roll(h[0], q - 1, 0))
        t = [t0, h[1], h[2], t3]
        save(w, m, t)
        for p in range(4):
            at = 4 * slot + p
            lo = jnp.where(lane == at, pltpu.roll(t[p][:, :LANES], at, 1), lo)
            hi = jnp.where(lane == at, pltpu.roll(t[p][:, half:], at + 1, 1), hi)
        return lo, hi

    def halo_copies(k):
        plan = [
            (col_tx.at[k, 0, pl.ds(0, 1)], cor_rx.at[k, 3], (up, left)),
            (col_tx.at[k, 1, pl.ds(0, 1)], cor_rx.at[k, 2], (up, right)),
            (col_tx.at[k, 0, pl.ds(q - 1, 1)], cor_rx.at[k, 1], (down, left)),
            (col_tx.at[k, 1, pl.ds(q - 1, 1)], cor_rx.at[k, 0], (down, right)),
            (row_tx.at[k, 0], row_rx.at[k, 1], (up, me_s)),
            (row_tx.at[k, 1], row_rx.at[k, 0], (down, me_s)),
            (col_tx.at[k, 0], col_rx.at[k, 1], (me_c, left)),
            (col_tx.at[k, 1], col_rx.at[k, 0], (me_c, right)),
        ]
        return [
            pltpu.make_async_remote_copy(
                src_ref=src, dst_ref=dst, send_sem=htx_sem.at[k, e], recv_sem=hrx_sem.at[k, e],
                device_id=where, device_id_type=MESH)
            for e, (src, dst, where) in enumerate(plan)
        ]

    def send(k, tops):
        col_tx[k, 0], col_tx[k, 1] = tops
        for copy in halo_copies(k):
            copy.start()

    def arrive(k):
        for copy in halo_copies(k):
            copy.wait_recv()
        ph = lax.broadcasted_iota(jnp.int32, (1, LANES), 1) % 4
        edge_row = lax.broadcasted_iota(jnp.int32, (q, LANES), 0)
        merged = []
        for side in range(2):
            above, below = cor_rx[k, side], cor_rx[k, 2 + side]
            above = jnp.where(ph == 0, pltpu.roll(above, LANES - 3, 1), 0.0)
            below = jnp.where(ph == 3, pltpu.roll(below, 3, 1), 0.0)
            c = col_rx[k, side]
            c = c + jnp.where(edge_row == 0, above, 0.0) + jnp.where(edge_row == q - 1, below, 0.0)
            merged.append(c)
        return merged

    def assembled(k, m, slot, merged):
        t = load(w, m)
        t[0] = t[0] + jnp.where(row_at == 0, row_rx[k, 0, pl.ds(slot, 1), :], 0.0)
        t[3] = t[3] + jnp.where(row_at == q - 1, row_rx[k, 1, pl.ds(slot, 1), :], 0.0)
        out = []
        for p in range(4):
            at = 4 * slot + p
            c = t[p] + jnp.where(
                take_next, pltpu.roll(t[p], cols - 1, 1),
                jnp.where(take_prev, pltpu.roll(t[p], 1, 1), 0.0))
            a = jnp.where(lane == 0, pltpu.roll(merged[0], LANES - at, 1), 0.0)
            b = jnp.where(lane == LANES - 1, pltpu.roll(merged[1], LANES - 1 - at, 1), 0.0)
            pieces = [c[:, e * LANES:(e + 1) * LANES] for e in range(tiles)]
            pieces[0] = pieces[0] + a
            pieces[-1] = pieces[-1] + b
            out.append(jnp.concatenate(pieces, axis=1))
        return out

    edge_w, mid_w = f32(1.0 / 6.0), f32(5.0 / 6.0)
    col_w = jnp.where(on_edge, edge_w, mid_w)
    mw, fw = [], []
    for copy in loads:
        copy.wait()
    for p in range(4):
        grid_w = col_w * (edge_w if p in (0, 3) else mid_w)
        mw.append(strided([factors.at[0, c] for c in range(tiles)], p, q) * grid_w)
        fw.append(strided([factors.at[1, c] for c in range(tiles)], p, q) * grid_w)
        mass[p * q:(p + 1) * q, :] = mw[p]
        flux[p * q:(p + 1) * q, :] = fw[p]
    zero = jnp.zeros((q, LANES), f32)
    tops = pack(0, modes, per, mw, (zero, zero))
    div_load.wait()
    table = div_ref[:cols, :].astype(f32) + div_ref[2 * cols:, :].astype(f32)
    by_cols = jnp.dot(flux[...], table * table, precision=lax.Precision.HIGHEST,
                      preferred_element_type=f32)
    squared = SLOPES * SLOPES
    lap = [combo(squared[:, a], fw) + by_cols[a * q:(a + 1) * q, :] for a in range(4)]
    tops = pack(0, modes + 1, per + 1, lap, tops)
    for copy in sources:
        copy.wait()
    for g in range(groups):

        def start_body(slot, carry, g=g):
            m = g * per + slot
            h = [strided([source.at[c, m] for c in range(tiles)], p, q)
                 * mass[p * q:(p + 1) * q, :] for p in range(4)]
            return pack(g, m, slot, h, carry)

        tops = lax.fori_loop(0, per, start_body, tops if g == 0 else (zero, zero), unroll=UNROLL)
        if g == 0:
            pl.semaphore_wait(barrier, n - 1)
        send(g, tops)
    scale_load.wait()
    grad_load.wait()

    pad = (lax.broadcasted_iota(jnp.int32, (1, LANES), 1) >= per).astype(f32)
    eye = lax.broadcasted_iota(jnp.int32, (slots, LANES), 0) == lax.broadcasted_iota(
        jnp.int32, (slots, LANES), 1)

    def update(it, g, m, slot, ww):
        a, b = coef[g, 0, pl.ds(slot, 1), :], coef[g, 1, pl.ds(slot, 1), :]
        zz = load(z, m)
        if it > 1:
            dd, ss = load(d, m), load(s, m)
            zz = [u + b * v for u, v in zip(zz, dd)]
            ww = [u + b * v for u, v in zip(ww, ss)]
            xx = [u + a * v for u, v in zip(load(x, m), zz)]
        else:
            xx = [a * v for v in zz]
        rr = [u - a * v for u, v in zip(load(r, m), ww)]
        return zz, ww, xx, rr

    def fill(slot, parts):
        v = jnp.concatenate(parts, axis=0)
        top = v.astype(bf16)
        at = pl.ds(pl.multiple_of(slot * rows, rows), rows)
        zcat[at, :cols] = top
        zcat[at, cols:] = (v - top.astype(f32)).astype(bf16)

    def multiply(table_ref):
        gout[...] = (
            jnp.dot(zcat[...], table_ref[:2 * cols, :], preferred_element_type=f32)
            + jnp.dot(zcat[:, :cols], table_ref[2 * cols:, :], preferred_element_type=f32))

    old = [None] * groups

    def coefficients(it, g):
        k = it * groups + g
        gathered = ar_rx.at[k, pl.ds(1, n - 1)]
        pltpu.make_async_copy(gathered, gathered, arx_sem.at[k]).wait()
        total = jnp.sum(ar_rx[k], axis=0)
        rho, curve_sum = total[0:1] + pad, total[1:2] + pad
        if it == 0:
            mixing = jnp.zeros_like(rho)
            step_len = rho / curve_sum
        else:
            mixing = rho / old[g][0]
            step_len = rho / (curve_sum - mixing * rho / old[g][1])
        for e, line in enumerate((step_len, mixing)):
            tall = jnp.sum(jnp.where(eye, line, 0.0), axis=1, keepdims=True)
            coef[g, e] = jnp.broadcast_to(tall, (slots, cols))
        old[g] = (rho, step_len)

    for it in range(ITERS):
        for g in range(groups):
            base = g * per
            k = it * groups + g
            merged = arrive(k)
            if it == 0 and g == 0:
                for e in range(2):
                    save(w, modes + e, assembled(k, modes + e, per + e, merged))
            if it > 0:
                coefficients(it - 1, g)

            def first(slot, carry, it=it, g=g, k=k, base=base, merged=merged):
                m = base + slot
                ww = assembled(k, m, slot, merged)
                if it == 0:
                    rr = ww
                    inv = [1.0 / (u + scale_ref[m] * v)
                           for u, v in zip(load(w, modes), load(w, modes + 1))]
                    save(invp, m, inv)
                else:
                    dd, ss, xx, rr = update(it, g, m, slot, ww)
                    save(x, m, xx)
                    save(d, m, dd)
                    save(s, m, ss)
                    inv = load(invp, m)
                save(r, m, rr)
                zz = [u * v for u, v in zip(rr, inv)]
                save(z, m, zz)
                fill(slot, zz)
                rz = [u * v for u, v in zip(rr, zz)]
                rho = (rz[0] + rz[3]) * 0.5 + (rz[1] + rz[2])
                rho = jnp.where(on_edge, rho * 0.5, rho)
                sums[0, pl.ds(slot, 1), :] = jnp.sum(rho, axis=0, keepdims=True)
                f = load2(flux)
                fg = [f[a] * combo(SLOPES[a], zz) * scale_ref[m] for a in range(4)]
                ms = load2(mass)
                save(w, m, [ms[a] * zz[a] + combo(SLOPES[:, a], fg) for a in range(4)])
                return carry

            lax.fori_loop(0, per, first, 0, unroll=UNROLL)
            multiply(grad_ref)

            def second(slot, carry, base=base):
                grad = gout[pl.ds(pl.multiple_of(slot * rows, rows), rows), :]
                fill(slot, [flux[...] * grad * scale_ref[base + slot]])
                return carry

            lax.fori_loop(0, per, second, 0, unroll=UNROLL)
            multiply(div_ref)

            def third(slot, carry, k=k, base=base):
                m = base + slot
                zz = load(z, m)
                h = [u + gout[pl.ds(pl.multiple_of(slot * rows + p * q, q), q), :]
                     for p, u in enumerate(load(w, m))]
                zh = zz[0] * h[0] + zz[1] * h[1] + zz[2] * h[2] + zz[3] * h[3]
                sums[1, pl.ds(slot, 1), :] = jnp.sum(zh, axis=0, keepdims=True)
                return pack(k + groups, m, slot, h, carry)

            tops = lax.fori_loop(0, per, third, (zero, zero), unroll=UNROLL)
            send(k + groups, tops)
            for e in range(2):
                part = jnp.sum(sums[e], axis=1, keepdims=True)
                line = jnp.sum(jnp.where(eye, part, 0.0), axis=0, keepdims=True)
                ar_tx[k, e:e + 1, :] = line
                ar_rx[k, 0, e:e + 1, :] = line

            def spread(offset, carry, k=k):
                pltpu.make_async_remote_copy(
                    src_ref=ar_tx.at[k], dst_ref=ar_rx.at[k, offset],
                    send_sem=atx_sem.at[k], recv_sem=arx_sem.at[k],
                    device_id=place(offset), device_id_type=MESH).start()
                return carry

            lax.fori_loop(1, n, spread, 0)

    for g in range(groups):
        k = ITERS * groups + g
        merged = arrive(k)
        coefficients(ITERS - 1, g)

        def last(slot, carry, g=g, k=k, merged=merged):
            m = g * per + slot
            _, _, xx, rr = update(ITERS, g, m, slot, assembled(k, m, slot, merged))
            save(x, m, xx)
            save(r, m, rr)
            return carry

        lax.fori_loop(0, per, last, 0, unroll=UNROLL)

    for k in range((ITERS + 1) * groups):
        for copy in halo_copies(k):
            copy.wait_send()
    for k in range(ITERS * groups):
        sent = ar_rx.at[k, pl.ds(1, n - 1)]
        pltpu.make_async_copy(sent, sent, atx_sem.at[k]).wait()


def node_order(x, r, sol_ref, res_ref, sol_buf, res_buf, sem):
    modes, rows, cols = x.shape
    q, tiles = rows // 4, cols // LANES

    def stores(m):
        return [
            pltpu.make_async_copy(
                buf.at[c, m], out.at[m, :, pl.ds(c * LANES, LANES)], sem.at[k, c, m])
            for k, (buf, out) in enumerate(((sol_buf, sol_ref), (res_buf, res_ref)))
            for c in range(tiles)
        ]

    def body(m, carry):
        for c in range(tiles):
            for p in range(4):
                cut = slice(c * LANES, (c + 1) * LANES)
                sol_buf[c, m, pl.ds(p, q, stride=4), :] = x[m, p * q:(p + 1) * q, cut]
                res_buf[c, m, pl.ds(p, q, stride=4), :] = r[m, p * q:(p + 1) * q, cut]
        for copy in stores(m):
            copy.start()
        return carry

    lax.fori_loop(0, modes, body, 0)

    def drain(m, carry):
        for copy in stores(m):
            copy.wait()
        return carry

    lax.fori_loop(0, modes, drain, 0)


def strided(refs, p, q):
    return jnp.concatenate([ref[pl.ds(p, q, stride=4), :] for ref in refs], axis=1)


def stack_table(table):
    top = table.astype(bf16)
    low = (table - top.astype(np.float32)).astype(bf16)
    return np.concatenate([top, top, low], axis=0)


def shards(nc, ns, forcing, metric, jacobian, mode_scale):
    modes, rows, cols = forcing.shape
    block = np.kron(np.eye(cols // 4), SLOPES).astype(np.float32)
    grad, div = stack_table(block.T), stack_table(block)
    n, q, tiles = nc * ns, rows // 4, cols // LANES
    groups = GROUPS if modes % GROUPS == 0 else 1
    per = modes // groups
    slots = -(-(per + 2) // 8) * 8
    vm = pl.BlockSpec(memory_space=pltpu.VMEM)
    hbm = pl.BlockSpec(memory_space=pltpu.HBM)
    rounds, sums = (ITERS + 1) * groups, ITERS * groups
    field = pltpu.VMEM((modes, rows, cols), f32)
    split = pltpu.VMEM((tiles, modes, rows, LANES), f32)
    table = pltpu.VMEM(grad.shape, bf16)
    shape = jax.ShapeDtypeStruct(forcing.shape, f32)
    x, r = pl.pallas_call(
        functools.partial(kernel, nc, ns, modes, groups),
        out_shape=[shape] * 2,
        in_specs=[hbm] * 6,
        out_specs=[vm, vm],
        scratch_shapes=[
            field, field, field,
            pltpu.VMEM((modes + 2, rows, cols), f32),
            field,
            pltpu.VMEM((rows, cols), f32),
            pltpu.VMEM((rows, cols), f32),
            pltpu.VMEM((per * rows, 2 * cols), bf16),
            pltpu.VMEM((per * rows, cols), f32),
            pltpu.VMEM((2, slots, cols), f32),
            pltpu.VMEM((groups, 2, slots, cols), f32),
            pltpu.VMEM((rounds, 2, slots, cols), f32),
            pltpu.VMEM((rounds, 2, slots, cols), f32),
            pltpu.VMEM((rounds, 2, q, LANES), f32),
            pltpu.VMEM((rounds, 2, q, LANES), f32),
            pltpu.VMEM((rounds, 4, 1, LANES), f32),
            pltpu.VMEM((sums, 2, LANES), f32),
            pltpu.VMEM((sums, n, 2, LANES), f32),
            split,
            pltpu.VMEM((2, tiles, rows, LANES), f32),
            table, table,
            pltpu.SMEM((modes,), f32),
            pltpu.SemaphoreType.DMA((rounds, 8)),
            pltpu.SemaphoreType.DMA((rounds, 8)),
            pltpu.SemaphoreType.DMA((sums,)),
            pltpu.SemaphoreType.DMA((sums,)),
            pltpu.SemaphoreType.DMA((3, tiles)),
            pltpu.SemaphoreType.DMA((3,)),
        ],
        compiler_params=pltpu.CompilerParams(
            collective_id=0, has_side_effects=True, vmem_limit_bytes=41943040),
    )(*[pltpu.with_memory_space_constraint(v, pltpu.HBM) for v in (mode_scale, forcing, metric, jacobian, jnp.asarray(grad), jnp.asarray(div))])
    return pl.pallas_call(
        node_order,
        out_shape=[shape] * 2,
        in_specs=[vm, vm],
        out_specs=[hbm, hbm],
        scratch_shapes=[split, split, pltpu.SemaphoreType.DMA((2, tiles, modes))],
        compiler_params=pltpu.CompilerParams(vmem_limit_bytes=16 * 1024 * 1024),
    )(x, r)


def solution(mesh):
    placed = (P(None, "curve", "sub"), P("curve", "sub"), P("curve", "sub"), P())
    return jax.shard_map(
        functools.partial(shards, mesh.shape["curve"], mesh.shape["sub"]),
        mesh=mesh,
        in_specs=placed,
        out_specs=(P(None, "curve", "sub"), P(None, "curve", "sub")),
        check_vma=False,
    )
```

profile of v0, /device:TPU:1, one launch (start us, length us, event | category | flops | bytes accessed | tf_op | source)
XLA Modules:
  0.0 73.2 jit_solution(10780680094015022612)
XLA Ops:
  0.6 70.8 %shard_map.77 = (f32[12,96,256]{2,1,0:T(8,128)S(1)}, f32[12,96,256]{2,1,0:T(8,128)S(1)}) custom-call(f32[12]{0:T(128)} %scale_hbm.1, f32[12,96,256]{2,1,0:T(8,128)} %forcing_ref.1, f32[96,256]{1,0:T(8,128)} %metric_ref.1, f32[96,256]{1,0:T(8,128)} %jac_ref.1, bf16[768,256]{1,0:T(8,128)(2,1)} %constant.4.clone.grad_hbm, bf16[768,256]{1,0:T(8,128)(2,1)} %constant.5.clone.div_hbm), custom_call_target="tpu_custom_call" | custom-call | tf_op jit(solution)/shard_map/pallas_call | solution.py:425
  71.4 1.8 %shard_map.78 = (f32[12,96,256]{2,1,0:T(8,128)}, f32[12,96,256]{2,1,0:T(8,128)}) custom-call(f32[12,96,256]{2,1,0:T(8,128)S(1)} %get-tuple-element.4.x, f32[12,96,256]{2,1,0:T(8,128)S(1)} %get-tuple-element.5.r), custom_call_target="tpu_custom_call" | custom-call | tf_op jit(solution)/shard_map/pallas_call | solution.py:461
where the time goes:
time: 73.3 us; the launch traced here: 73.2 us
  Pallas kernels  72.6 us (99%)
    pallas_call x1, Pallas kernels, shards(): pl.pallas_call(functools.partial(kernel, nc, ns, modes, groups), out_shap...  70.8 us
    pallas_call x1, Pallas kernels, shards(): pl.pallas_call(node_order, out_shape=[shape] * 2, in_specs=[vm, vm], out_...  1.8 us

commit v1 on v0

--- a/solution.py
+++ b/solution.py
@@ -46,22 +46,29 @@
     return total
 
 
+PRODUCTS = 6
+FIELD = 16
+
+
+def planes(nc, ns):
+    depth = 8 if nc % 16 == 0 else 2
+    return nc // (2 * depth), depth, 2, ns
+
+
 def kernel(
     nc, ns, modes, groups,
     scale_hbm, forcing_ref, metric_ref, jac_ref, grad_hbm, div_hbm,
-    x, r,
-    z, d, s, w, invp, mass, flux, zcat, gout, sums, coef,
-    row_tx, row_rx, col_tx, col_rx, cor_rx, ar_tx, ar_rx,
+    r0, r1, r2, u2, invp, coef,
+    z, w, mass, flux, zcat, gout, sums,
+    row_tx, row_rx, col_tx, col_rx, cor_rx, near_tx, near_rx, far_tx, far_rx,
     source, factors, grad_ref, div_ref, scale_ref,
     htx_sem, hrx_sem, atx_sem, arx_sem, in_sem, table_sem,
 ):
     rows, cols = metric_ref.shape
     q = rows // 4
-    n = nc * ns
     half = cols - LANES
     tiles = cols // LANES
     per = modes // groups
-    slots = row_tx.shape[2]
     loads, sources = [], []
     for c in range(tiles):
         cut = pl.ds(c * LANES, LANES)
@@ -78,21 +85,30 @@
         copy.start()
 
     me_c, me_s = lax.axis_index("curve"), lax.axis_index("sub")
-    me = me_c * ns + me_s
     up, down = lax.rem(me_c + nc - 1, nc), lax.rem(me_c + 1, nc)
     left, right = lax.rem(me_s + ns - 1, ns), lax.rem(me_s + 1, ns)
 
-    def place(offset):
-        target = lax.rem(me + offset, n)
-        return (target // ns, lax.rem(target, ns))
+    ny, nz, nk, nx = planes(nc, ns)
+    core, chip = lax.rem(me_c, nk), me_c // nk
+    at_z, at_y = lax.rem(chip, nz), chip // nz
+    subs = [me_s if dx == 0 else lax.rem(me_s + dx, nx) for dx in range(nx)]
+    near, far = [], []
+    for dy in range(ny):
+        y = at_y if dy == 0 else lax.rem(at_y + dy, ny)
+        for dk in range(nk):
+            k = core if dk == 0 else 1 - core
+            c = (y * nz + at_z) * nk + k
+            near += [(c, subs[dx]) for dx in range(nx)]
+    for dz in range(nz):
+        far.append(((at_y * nz + lax.rem(at_z + dz, nz)) * nk + core, me_s))
+    near, far = near[1:], far[1:]
 
     barrier = pltpu.get_barrier_semaphore()
-
-    def greet(offset, carry):
-        pl.semaphore_signal(barrier, inc=1, device_id=place(offset), device_id_type=MESH)
-        return carry
-
-    lax.fori_loop(1, n, greet, 0)
+    greeted = [
+        (up, left), (up, right), (down, left), (down, right), (up, me_s), (down, me_s),
+        (me_c, left), (me_c, right)] + near + far
+    for where in greeted:
+        pl.semaphore_signal(barrier, inc=1, device_id=where, device_id_type=MESH)
 
     lane_full = lax.broadcasted_iota(jnp.int32, (q, cols), 1)
     lane = lax.broadcasted_iota(jnp.int32, (q, LANES), 1)
@@ -214,58 +230,44 @@
 
         tops = lax.fori_loop(0, per, start_body, tops if g == 0 else (zero, zero), unroll=UNROLL)
         if g == 0:
-            pl.semaphore_wait(barrier, n - 1)
+            pl.semaphore_wait(barrier, len(greeted))
         send(g, tops)
     scale_load.wait()
     grad_load.wait()
 
-    pad = (lax.broadcasted_iota(jnp.int32, (1, LANES), 1) >= per).astype(f32)
-    eye = lax.broadcasted_iota(jnp.int32, (slots, LANES), 0) == lax.broadcasted_iota(
-        jnp.int32, (slots, LANES), 1)
-
-    def update(it, g, m, slot, ww):
-        a, b = coef[g, 0, pl.ds(slot, 1), :], coef[g, 1, pl.ds(slot, 1), :]
-        zz = load(z, m)
-        if it > 1:
-            dd, ss = load(d, m), load(s, m)
-            zz = [u + b * v for u, v in zip(zz, dd)]
-            ww = [u + b * v for u, v in zip(ww, ss)]
-            xx = [u + a * v for u, v in zip(load(x, m), zz)]
-        else:
-            xx = [a * v for v in zz]
-        rr = [u - a * v for u, v in zip(load(r, m), ww)]
-        return zz, ww, xx, rr
-
-    def fill(slot, parts):
+    def fill(g, slot, parts):
         v = jnp.concatenate(parts, axis=0)
         top = v.astype(bf16)
         at = pl.ds(pl.multiple_of(slot * rows, rows), rows)
-        zcat[at, :cols] = top
-        zcat[at, cols:] = (v - top.astype(f32)).astype(bf16)
-
-    def multiply(table_ref):
+        zcat[g, at, :cols] = top
+        zcat[g, at, cols:] = (v - top.astype(f32)).astype(bf16)
+
+    def multiply(g, table_ref):
         gout[...] = (
-            jnp.dot(zcat[...], table_ref[:2 * cols, :], preferred_element_type=f32)
-            + jnp.dot(zcat[:, :cols], table_ref[2 * cols:, :], preferred_element_type=f32))
-
-    old = [None] * groups
-
-    def coefficients(it, g):
-        k = it * groups + g
-        gathered = ar_rx.at[k, pl.ds(1, n - 1)]
-        pltpu.make_async_copy(gathered, gathered, arx_sem.at[k]).wait()
-        total = jnp.sum(ar_rx[k], axis=0)
-        rho, curve_sum = total[0:1] + pad, total[1:2] + pad
-        if it == 0:
-            mixing = jnp.zeros_like(rho)
-            step_len = rho / curve_sum
-        else:
-            mixing = rho / old[g][0]
-            step_len = rho / (curve_sum - mixing * rho / old[g][1])
-        for e, line in enumerate((step_len, mixing)):
-            tall = jnp.sum(jnp.where(eye, line, 0.0), axis=1, keepdims=True)
-            coef[g, e] = jnp.broadcast_to(tall, (slots, cols))
-        old[g] = (rho, step_len)
+            jnp.dot(zcat[g], table_ref[:2 * cols, :], preferred_element_type=f32)
+            + jnp.dot(zcat[g, :, :cols], table_ref[2 * cols:, :], preferred_element_type=f32))
+
+    def total_rows(parts):
+        return jnp.sum((parts[0] + parts[3]) + (parts[1] + parts[2]), axis=0, keepdims=True)
+
+    def shared_rows(parts):
+        line = (parts[0] + parts[3]) * 0.5 + (parts[1] + parts[2])
+        return jnp.sum(jnp.where(on_edge, line * 0.5, line), axis=0, keepdims=True)
+
+    def finish(g, k, base):
+        multiply(g, div_ref)
+
+        def third(slot, carry):
+            m = base + slot
+            h = [u + gout[pl.ds(pl.multiple_of(slot * rows + p * q, q), q), :]
+                 for p, u in enumerate(load(w, m))]
+            if k < ITERS - 1:
+                zh = [u * v for u, v in zip(load(z, m), h)]
+                sums[2 * k + 1, pl.ds(m, 1), :] = total_rows(zh)
+            return pack((k + 1) * groups + g, m, slot, h, carry)
+
+        tops = lax.fori_loop(0, per, third, (zero, zero), unroll=UNROLL)
+        send((k + 1) * groups + g, tops)
 
     for it in range(ITERS):
         for g in range(groups):
@@ -275,98 +277,132 @@
             if it == 0 and g == 0:
                 for e in range(2):
                     save(w, modes + e, assembled(k, modes + e, per + e, merged))
-            if it > 0:
-                coefficients(it - 1, g)
 
             def first(slot, carry, it=it, g=g, k=k, base=base, merged=merged):
                 m = base + slot
-                ww = assembled(k, m, slot, merged)
+                uu = assembled(k, m, slot, merged)
                 if it == 0:
-                    rr = ww
+                    rr = uu
                     inv = [1.0 / (u + scale_ref[m] * v)
                            for u, v in zip(load(w, modes), load(w, modes + 1))]
                     save(invp, m, inv)
+                    save(r0, m, rr)
+                elif it == 1:
+                    rr = [u - v for u, v in zip(uu, load(r0, m))]
+                    inv = load(invp, m)
+                    save(r1, m, rr)
                 else:
-                    dd, ss, xx, rr = update(it, g, m, slot, ww)
-                    save(x, m, xx)
-                    save(d, m, dd)
-                    save(s, m, ss)
+                    rr = [2.0 * (u - v) - s for u, v, s in zip(uu, load(r1, m), load(r0, m))]
                     inv = load(invp, m)
-                save(r, m, rr)
+                    save(r2, m, rr)
                 zz = [u * v for u, v in zip(rr, inv)]
-                save(z, m, zz)
-                fill(slot, zz)
-                rz = [u * v for u, v in zip(rr, zz)]
-                rho = (rz[0] + rz[3]) * 0.5 + (rz[1] + rz[2])
-                rho = jnp.where(on_edge, rho * 0.5, rho)
-                sums[0, pl.ds(slot, 1), :] = jnp.sum(rho, axis=0, keepdims=True)
+                fill(g, slot, zz)
+                sums[2 * it, pl.ds(m, 1), :] = shared_rows([u * v for u, v in zip(uu, zz)])
                 f = load2(flux)
-                fg = [f[a] * combo(SLOPES[a], zz) * scale_ref[m] for a in range(4)]
-                ms = load2(mass)
-                save(w, m, [ms[a] * zz[a] + combo(SLOPES[:, a], fg) for a in range(4)])
+                gx = [combo(SLOPES[a], zz) for a in range(4)]
+                fg = [f[a] * gx[a] * scale_ref[m] for a in range(4)]
+                mz = [u * v for u, v in zip(load2(mass), zz)]
+                if it < ITERS - 1:
+                    save(z, m, zz)
+                else:
+                    sums[2 * it + 1, pl.ds(m, 1), :] = total_rows(
+                        [u * v + s * t for u, v, s, t in zip(mz, zz, fg, gx)])
+                save(w, m, [mz[a] + combo(SLOPES[:, a], fg) for a in range(4)])
                 return carry
 
             lax.fori_loop(0, per, first, 0, unroll=UNROLL)
-            multiply(grad_ref)
-
-            def second(slot, carry, base=base):
-                grad = gout[pl.ds(pl.multiple_of(slot * rows, rows), rows), :]
-                fill(slot, [flux[...] * grad * scale_ref[base + slot]])
+            multiply(g, grad_ref)
+
+            def second(slot, carry, it=it, g=g, base=base):
+                m = base + slot
+                grad = [gout[pl.ds(pl.multiple_of(slot * rows + p * q, q), q), :]
+                        for p in range(4)]
+                fy = [u * v * scale_ref[m] for u, v in zip(load2(flux), grad)]
+                if it == ITERS - 1:
+                    e = 2 * it + 1
+                    sums[e, pl.ds(m, 1), :] = sums[e, pl.ds(m, 1), :] + total_rows(
+                        [u * v for u, v in zip(fy, grad)])
+                fill(g, slot, fy)
                 return carry
 
             lax.fori_loop(0, per, second, 0, unroll=UNROLL)
-            multiply(div_ref)
-
-            def third(slot, carry, k=k, base=base):
-                m = base + slot
-                zz = load(z, m)
-                h = [u + gout[pl.ds(pl.multiple_of(slot * rows + p * q, q), q), :]
-                     for p, u in enumerate(load(w, m))]
-                zh = zz[0] * h[0] + zz[1] * h[1] + zz[2] * h[2] + zz[3] * h[3]
-                sums[1, pl.ds(slot, 1), :] = jnp.sum(zh, axis=0, keepdims=True)
-                return pack(k + groups, m, slot, h, carry)
-
-            tops = lax.fori_loop(0, per, third, (zero, zero), unroll=UNROLL)
-            send(k + groups, tops)
-            for e in range(2):
-                part = jnp.sum(sums[e], axis=1, keepdims=True)
-                line = jnp.sum(jnp.where(eye, part, 0.0), axis=0, keepdims=True)
-                ar_tx[k, e:e + 1, :] = line
-                ar_rx[k, 0, e:e + 1, :] = line
-
-            def spread(offset, carry, k=k):
-                pltpu.make_async_remote_copy(
-                    src_ref=ar_tx.at[k], dst_ref=ar_rx.at[k, offset],
-                    send_sem=atx_sem.at[k], recv_sem=arx_sem.at[k],
-                    device_id=place(offset), device_id_type=MESH).start()
-                return carry
-
-            lax.fori_loop(1, n, spread, 0)
-
+            if it < ITERS - 1:
+                finish(g, it, base)
+
+    high = lax.broadcasted_iota(jnp.int32, (FIELD, LANES), 0)
+    wide = lax.broadcasted_iota(jnp.int32, (FIELD, LANES), 1)
+    picks = [(wide == e * FIELD + high) & (high < modes) for e in range(PRODUCTS)]
+    spread = jnp.zeros((FIELD, LANES), f32)
+    for e in range(PRODUCTS):
+        part = jnp.sum(sums[e], axis=1, keepdims=True)
+        spread = spread + jnp.where(picks[e], part, 0.0)
+    line = jnp.sum(spread, axis=0, keepdims=True)
+
+    def share(stage, line, tx, rx, peers):
+        tx[...] = line
+        rx[0] = line
+        for j, where in enumerate(peers):
+            pltpu.make_async_remote_copy(
+                src_ref=tx, dst_ref=rx.at[j + 1], send_sem=atx_sem.at[stage],
+                recv_sem=arx_sem.at[stage], device_id=where, device_id_type=MESH).start()
+
+    def gather(stage, rx):
+        got = rx.at[pl.ds(1, rx.shape[0] - 1)]
+        pltpu.make_async_copy(got, got, arx_sem.at[stage]).wait()
+        return jnp.sum(rx[...], axis=0)
+
+    share(0, line, near_tx, near_rx, near)
+    for g in range(groups):
+        finish(g, ITERS - 1, g * per)
+    share(1, gather(0, near_rx), far_tx, far_rx, far)
     for g in range(groups):
         k = ITERS * groups + g
         merged = arrive(k)
-        coefficients(ITERS - 1, g)
 
         def last(slot, carry, g=g, k=k, merged=merged):
             m = g * per + slot
-            _, _, xx, rr = update(ITERS, g, m, slot, assembled(k, m, slot, merged))
-            save(x, m, xx)
-            save(r, m, rr)
+            save(u2, m, assembled(k, m, slot, merged))
             return carry
 
         lax.fori_loop(0, per, last, 0, unroll=UNROLL)
+
+    total = gather(1, far_rx)
+    pad = (high[:, :1] >= modes).astype(f32)
+    n0, p00, p01, p11, p12, p22 = [
+        jnp.broadcast_to(
+            jnp.sum(jnp.where(pick, total, 0.0), axis=1, keepdims=True), (FIELD, LANES))
+        for pick in picks]
+    pad = jnp.broadcast_to(pad, (FIELD, LANES))
+    p00, p11, p22 = p00 + pad, p11 + pad, p22 + 2.0 * pad
+    b0 = n0
+    b1 = p00 - n0
+    b2 = 2.0 * (p01 - b1) - n0
+    p02 = 2.0 * p11 - p00
+    i0 = 1.0 / p00
+    l1, l2 = p01 * i0, p02 * i0
+    d1 = p11 - l1 * p01
+    t2 = p12 - l2 * p01
+    i1 = 1.0 / d1
+    l3 = t2 * i1
+    d2 = p22 - l2 * p02 - l3 * t2
+    y1 = b1 - l1 * b0
+    y2 = b2 - l2 * b0 - l3 * y1
+    c2 = y2 / d2
+    c1 = y1 * i1 - l3 * c2
+    c0 = b0 * i0 - l1 * c1 - l2 * c2
+    for e, c in enumerate((c0, c1, c2, 1.0 - c0 - 0.5 * c1, c0 + c1, 0.5 * c1)):
+        coef[e] = c
 
     for k in range((ITERS + 1) * groups):
         for copy in halo_copies(k):
             copy.wait_send()
-    for k in range(ITERS * groups):
-        sent = ar_rx.at[k, pl.ds(1, n - 1)]
-        pltpu.make_async_copy(sent, sent, atx_sem.at[k]).wait()
-
-
-def node_order(x, r, sol_ref, res_ref, sol_buf, res_buf, sem):
-    modes, rows, cols = x.shape
+    for stage, rx in enumerate((near_rx, far_rx)):
+        sent = rx.at[pl.ds(1, rx.shape[0] - 1)]
+        pltpu.make_async_copy(sent, sent, atx_sem.at[stage]).wait()
+
+
+def node_order(r0, r1, r2, u2, invp, coef, sol_ref, res_ref, sol_buf, res_buf, sem):
+    modes, rows, cols = r0.shape
     q, tiles = rows // 4, cols // LANES
 
     def stores(m):
@@ -378,11 +414,14 @@
         ]
 
     def body(m, carry):
+        c0, c1, c2, e0, e1, e2 = [coef[e, pl.ds(m, 1), :] for e in range(6)]
         for c in range(tiles):
             for p in range(4):
-                cut = slice(c * LANES, (c + 1) * LANES)
-                sol_buf[c, m, pl.ds(p, q, stride=4), :] = x[m, p * q:(p + 1) * q, cut]
-                res_buf[c, m, pl.ds(p, q, stride=4), :] = r[m, p * q:(p + 1) * q, cut]
+                at = (m, slice(p * q, (p + 1) * q), slice(c * LANES, (c + 1) * LANES))
+                a0, a1, a2 = r0[at], r1[at], r2[at]
+                sol_buf[c, m, pl.ds(p, q, stride=4), :] = invp[at] * (c0 * a0 + c1 * a1 + c2 * a2)
+                res_buf[c, m, pl.ds(p, q, stride=4), :] = (
+                    e0 * a0 - e1 * a1 - e2 * a2 - c2 * u2[at])
         for copy in stores(m):
             copy.start()
         return carry
@@ -411,47 +450,49 @@
     modes, rows, cols = forcing.shape
     block = np.kron(np.eye(cols // 4), SLOPES).astype(np.float32)
     grad, div = stack_table(block.T), stack_table(block)
-    n, q, tiles = nc * ns, rows // 4, cols // LANES
+    q, tiles = rows // 4, cols // LANES
     groups = GROUPS if modes % GROUPS == 0 else 1
     per = modes // groups
     slots = -(-(per + 2) // 8) * 8
     vm = pl.BlockSpec(memory_space=pltpu.VMEM)
     hbm = pl.BlockSpec(memory_space=pltpu.HBM)
-    rounds, sums = (ITERS + 1) * groups, ITERS * groups
+    rounds = (ITERS + 1) * groups
+    ny, nz, nk, nx = planes(nc, ns)
     field = pltpu.VMEM((modes, rows, cols), f32)
     split = pltpu.VMEM((tiles, modes, rows, LANES), f32)
     table = pltpu.VMEM(grad.shape, bf16)
+    line = pltpu.VMEM((1, LANES), f32)
     shape = jax.ShapeDtypeStruct(forcing.shape, f32)
-    x, r = pl.pallas_call(
+    kept = pl.pallas_call(
         functools.partial(kernel, nc, ns, modes, groups),
-        out_shape=[shape] * 2,
+        out_shape=[shape] * 5 + [jax.ShapeDtypeStruct((6, FIELD, LANES), f32)],
         in_specs=[hbm] * 6,
-        out_specs=[vm, vm],
+        out_specs=[vm] * 6,
         scratch_shapes=[
-            field, field, field,
+            field,
             pltpu.VMEM((modes + 2, rows, cols), f32),
-            field,
             pltpu.VMEM((rows, cols), f32),
             pltpu.VMEM((rows, cols), f32),
-            pltpu.VMEM((per * rows, 2 * cols), bf16),
+            pltpu.VMEM((groups, per * rows, 2 * cols), bf16),
             pltpu.VMEM((per * rows, cols), f32),
-            pltpu.VMEM((2, slots, cols), f32),
-            pltpu.VMEM((groups, 2, slots, cols), f32),
+            pltpu.VMEM((PRODUCTS, FIELD, cols), f32),
             pltpu.VMEM((rounds, 2, slots, cols), f32),
             pltpu.VMEM((rounds, 2, slots, cols), f32),
             pltpu.VMEM((rounds, 2, q, LANES), f32),
             pltpu.VMEM((rounds, 2, q, LANES), f32),
             pltpu.VMEM((rounds, 4, 1, LANES), f32),
-            pltpu.VMEM((sums, 2, LANES), f32),
-            pltpu.VMEM((sums, n, 2, LANES), f32),
+            line,
+            pltpu.VMEM((ny * nk * nx, 1, LANES), f32),
+            line,
+            pltpu.VMEM((nz, 1, LANES), f32),
             split,
             pltpu.VMEM((2, tiles, rows, LANES), f32),
             table, table,
             pltpu.SMEM((modes,), f32),
             pltpu.SemaphoreType.DMA((rounds, 8)),
             pltpu.SemaphoreType.DMA((rounds, 8)),
-            pltpu.SemaphoreType.DMA((sums,)),
-            pltpu.SemaphoreType.DMA((sums,)),
+            pltpu.SemaphoreType.DMA((2,)),
+            pltpu.SemaphoreType.DMA((2,)),
             pltpu.SemaphoreType.DMA((3, tiles)),
             pltpu.SemaphoreType.DMA((3,)),
         ],
@@ -461,11 +502,11 @@
     return pl.pallas_call(
         node_order,
         out_shape=[shape] * 2,
-        in_specs=[vm, vm],
+        in_specs=[vm] * 6,
         out_specs=[hbm, hbm],
         scratch_shapes=[split, split, pltpu.SemaphoreType.DMA((2, tiles, modes))],
         compiler_params=pltpu.CompilerParams(vmem_limit_bytes=16 * 1024 * 1024),
-    )(x, r)
+    )(*kept)
 
 
 def solution(mesh):

time: 73.3 us -> 41.4 us (0.56)
  Pallas kernels: 72.6 us -> 40.7 us
    pallas_call x1, Pallas kernels: 70.8 us -> 38.9 us  [shards(): pl.pallas_call(functools.partial(kernel, nc, ns, modes, groups), out_shap...]
where the time goes in v1:
time: 41.4 us; the launch traced here: 41.3 us
  Pallas kernels  40.7 us (98%)
  between operations  0.64 us (2%)
    pallas_call x1, Pallas kernels, shards(): pl.pallas_call(functools.partial(kernel, nc, ns, modes, groups), out_shap...  38.9 us
    pallas_call x1, Pallas kernels, shards(): pl.pallas_call(node_order, out_shape=[shape] * 2, in_specs=[vm] * 6, out_...  1.82 us

profile of v1, /device:TPU:1, one launch (start us, length us, event | category | flops | bytes accessed | tf_op | source)
XLA Modules:
  0.0 41.3 jit_solution(12741951608447038042)
XLA Ops:
  0.6 38.9 %shard_map.77 = (f32[12,96,256]{2,1,0:T(8,128)S(1)}, f32[12,96,256]{2,1,0:T(8,128)S(1)}, f32[12,96,256]{2,1,0:T(8,128)S(1)}, f32[12,96,256]{2,1,0:T(8,128)S(1)},...) custom-call(f32[12]{0:T(128)} %scale_hbm.1, f32[12,96,256]{2,1,0:T(8,128)} %forcing_ref.1, f32[96,256]{1,0:T(8,128)} %metric_ref.1, ...), custom_call_target="tpu_custom_call" | custom-call | tf_op jit(solution)/shard_map/pallas_call | solution.py:466
  39.5 1.8 %shard_map.78 = (f32[12,96,256]{2,1,0:T(8,128)}, f32[12,96,256]{2,1,0:T(8,128)}) custom-call(f32[12,96,256]{2,1,0:T(8,128)S(1)} %get-tuple-element.8.r0, f32[12,96,256]{2,1,0:T(8,128)S(1)} %get-tuple-element.9.r1, f32[12,96,256]{2,1,0:T(8,128)S(1)} %get-tuple-element.10.r2, f32[12,96,256]{2,1,0:T(8,128)S(1)} %get-tuple-element.11.u2, ...), custom_call_target="tpu_custom_call" | custom-call | tf_op jit(solution)/shard_map/pallas_call | solution.py:502

commit v2 on v1

--- a/solution.py
+++ b/solution.py
@@ -10,7 +10,7 @@
 from jax.sharding import PartitionSpec as P
 
 ITERS = 3
-GROUPS = 2
+GROUPS = 3
 UNROLL = True
 MESH = pl.DeviceIdType.MESH
 LANES = 128

time: 41.4 us -> 41.9 us (1.012)
    pallas_call x1, Pallas kernels: 38.9 us -> 39.3 us  [shards(): pl.pallas_call(functools.partial(kernel, nc, ns, modes, groups), out_shap...]
where the time goes in v2:
time: 41.9 us; the launch traced here: 41.8 us
  Pallas kernels  41.1 us (98%)
  between operations  0.64 us (2%)
    pallas_call x1, Pallas kernels, shards(): pl.pallas_call(functools.partial(kernel, nc, ns, modes, groups), out_shap...  39.3 us
    pallas_call x1, Pallas kernels, shards(): pl.pallas_call(node_order, out_shape=[shape] * 2, in_specs=[vm] * 6, out_...  1.82 us

profile of v2, /device:TPU:1, one launch (start us, length us, event | category | flops | bytes accessed | tf_op | source)
XLA Modules:
  0.0 41.8 jit_solution(16007360857903171429)
XLA Ops:
  0.6 39.3 %shard_map.77 = (f32[12,96,256]{2,1,0:T(8,128)S(1)}, f32[12,96,256]{2,1,0:T(8,128)S(1)}, f32[12,96,256]{2,1,0:T(8,128)S(1)}, f32[12,96,256]{2,1,0:T(8,128)S(1)},...) custom-call(f32[12]{0:T(128)} %scale_hbm.1, f32[12,96,256]{2,1,0:T(8,128)} %forcing_ref.1, f32[96,256]{1,0:T(8,128)} %metric_ref.1, ...), custom_call_target="tpu_custom_call" | custom-call | tf_op jit(solution)/shard_map/pallas_call | solution.py:466
  40.0 1.8 %shard_map.78 = (f32[12,96,256]{2,1,0:T(8,128)}, f32[12,96,256]{2,1,0:T(8,128)}) custom-call(f32[12,96,256]{2,1,0:T(8,128)S(1)} %get-tuple-element.8.r0, f32[12,96,256]{2,1,0:T(8,128)S(1)} %get-tuple-element.9.r1, f32[12,96,256]{2,1,0:T(8,128)S(1)} %get-tuple-element.10.r2, f32[12,96,256]{2,1,0:T(8,128)S(1)} %get-tuple-element.11.u2, ...), custom_call_target="tpu_custom_call" | custom-call | tf_op jit(solution)/shard_map/pallas_call | solution.py:502

commit v3 on v1

--- a/solution.py
+++ b/solution.py
@@ -60,7 +60,7 @@
     scale_hbm, forcing_ref, metric_ref, jac_ref, grad_hbm, div_hbm,
     r0, r1, r2, u2, invp, coef,
     z, w, mass, flux, zcat, gout, sums,
-    row_tx, row_rx, col_tx, col_rx, cor_rx, near_tx, near_rx, far_tx, far_rx,
+    row_tx, row_rx, col_tx, col_rx, cor_tx, cor_rx, near_tx, near_rx, far_tx, far_rx,
     source, factors, grad_ref, div_ref, scale_ref,
     htx_sem, hrx_sem, atx_sem, arx_sem, in_sem, table_sem,
 ):
@@ -69,6 +69,7 @@
     half = cols - LANES
     tiles = cols // LANES
     per = modes // groups
+    slots = row_tx.shape[2]
     loads, sources = [], []
     for c in range(tiles):
         cut = pl.ds(c * LANES, LANES)
@@ -142,12 +143,19 @@
             hi = jnp.where(lane == at, pltpu.roll(t[p][:, half:], at + 1, 1), hi)
         return lo, hi
 
+    def early(k):
+        return groups <= k < ITERS * groups
+
     def halo_copies(k):
+        if early(k):
+            corners = [cor_tx.at[k, pl.ds(2 * e, 1)] for e in range(4)]
+        else:
+            corners = [col_tx.at[k, e % 2, pl.ds(0 if e < 2 else q - 1, 1)] for e in range(4)]
         plan = [
-            (col_tx.at[k, 0, pl.ds(0, 1)], cor_rx.at[k, 3], (up, left)),
-            (col_tx.at[k, 1, pl.ds(0, 1)], cor_rx.at[k, 2], (up, right)),
-            (col_tx.at[k, 0, pl.ds(q - 1, 1)], cor_rx.at[k, 1], (down, left)),
-            (col_tx.at[k, 1, pl.ds(q - 1, 1)], cor_rx.at[k, 0], (down, right)),
+            (corners[0], cor_rx.at[k, 3], (up, left)),
+            (corners[1], cor_rx.at[k, 2], (up, right)),
+            (corners[2], cor_rx.at[k, 1], (down, left)),
+            (corners[3], cor_rx.at[k, 0], (down, right)),
             (row_tx.at[k, 0], row_rx.at[k, 1], (up, me_s)),
             (row_tx.at[k, 1], row_rx.at[k, 0], (down, me_s)),
             (col_tx.at[k, 0], col_rx.at[k, 1], (me_c, left)),
@@ -162,7 +170,7 @@
 
     def send(k, tops):
         col_tx[k, 0], col_tx[k, 1] = tops
-        for copy in halo_copies(k):
+        for copy in halo_copies(k)[4 if early(k) else 0:]:
             copy.start()
 
     def arrive(k):
@@ -235,6 +243,105 @@
     scale_load.wait()
     grad_load.wait()
 
+    at_lane = lax.broadcasted_iota(jnp.int32, (1, LANES), 1)
+    of_four = at_lane % 4
+    tall = lax.broadcasted_iota(jnp.int32, (slots, LANES), 0)
+    flat = lax.broadcasted_iota(jnp.int32, (slots, LANES), 1)
+    low_half = tall < 4
+
+    def coefs(values):
+        line = jnp.zeros((1, LANES), f32)
+        for e, value in enumerate(values):
+            line = jnp.where(of_four == e, f32(value), line)
+        return line
+
+    def corner_weights(g):
+        scale = jnp.zeros((1, LANES), f32)
+        for slot in range(per):
+            scale = jnp.where(at_lane // 4 == slot, scale_ref[g * per + slot], scale)
+        lines = []
+        for tb in range(2):
+            er, cr = (0, 0) if tb == 0 else (q - 1, 3)
+            for side in range(2):
+                cc, edge, start = (0, 0, 0) if side == 0 else (3, cols - 1, cols - 4)
+                sx = jnp.zeros((1, LANES), f32)
+                sy = jnp.zeros((1, LANES), f32)
+                own = jnp.zeros((1, 1), f32)
+                for e in range(4):
+                    fx = flux[e * q + er:e * q + er + 1, edge:edge + 1]
+                    fy = flux[cr * q + er:cr * q + er + 1, start + e:start + e + 1]
+                    sx = sx + fx * coefs(SLOPES[e, cr] * SLOPES[e])
+                    sy = sy + fy * coefs(SLOPES[e, cc] * SLOPES[e])
+                    own = own + fy * f32(SLOPES[e, cc] * SLOPES[e, cc])
+                here = mass[cr * q + er:cr * q + er + 1, edge:edge + 1]
+                lines += [
+                    scale * sx + jnp.where(of_four == cr, here + scale * own, 0.0),
+                    jnp.where(of_four == cc, 0.0, scale * sy)]
+        return scale, jnp.concatenate(lines, axis=0)
+
+    def gathered_rows(x):
+        left = x[:, :LANES]
+        left = left + jnp.where(flat == 3, pltpu.roll(left, LANES - 1, 1), 0.0)
+        right = x[:, half:]
+        right = right + jnp.where(flat == LANES - 4, pltpu.roll(right, 1, 1), 0.0)
+        left = pltpu.roll(jnp.where(flat < 4, left, 0.0), 0, 1, stride=4, stride_axis=0)
+        right = pltpu.roll(
+            jnp.where(flat >= LANES - 4, right, 0.0), 4, 1, stride=4, stride_axis=0)
+        return [jnp.sum(v, axis=0, keepdims=True) for v in (left, right)]
+
+    def corner_values(k, merged):
+        lines = []
+        for tb in range(2):
+            er, cr = (0, 0) if tb == 0 else (q - 1, 3)
+            halo = row_rx[k, tb]
+            rows_here = gathered_rows(row_tx[k, tb] + halo)
+            for side in range(2):
+                edge = 0 if side == 0 else cols - 1
+                place = flat == 4 * tall + cr
+                extra = jnp.sum(
+                    jnp.where(place, halo[:, edge:edge + 1], 0.0), axis=0, keepdims=True)
+                col = col_tx[k, side, er:er + 1, :] + merged[side][er:er + 1, :] + extra
+                lines += [col, rows_here[side]]
+        return jnp.concatenate(lines, axis=0)
+
+    def send_corners(k, weights, v):
+        h = weights * v
+        fore = h + pltpu.roll(h, LANES - 1, 1)
+        fore = fore + pltpu.roll(fore, LANES - 2, 1)
+        back = h + pltpu.roll(h, 1, 1)
+        back = back + pltpu.roll(back, 2, 1)
+        h = jnp.where(low_half, fore, back)
+        cor_tx[k] = h + pltpu.roll(h, slots - 1, 0)
+        for copy in halo_copies(k)[:4]:
+            copy.start()
+
+    def repeat(x, slot):
+        x = jnp.where(flat // 4 == slot, x, 0.0)
+        x = pltpu.roll(x, LANES - 4 * slot, 1)
+        for step in (4, 8, 16):
+            x = x + pltpu.roll(x, step, 1)
+        return x
+
+    assert slots == 8
+    corner = [corner_weights(g) for g in range(groups)]
+    corner_r, corner_inv, shared_diag = [None] * groups, [None] * groups, []
+
+    def corner_step(it, g, k, merged):
+        u = corner_values(k, merged)
+        scale, weights = corner[g]
+        if it == 0:
+            if g == 0:
+                shared_diag.extend([repeat(u, per), repeat(u, per + 1)])
+            used = flat < 4 * per
+            u = jnp.where(used, u, 0.0)
+            corner_r[g] = u
+            corner_inv[g] = jnp.where(used, 1.0 / jnp.where(
+                used, shared_diag[0] + scale * shared_diag[1], 1.0), 0.0)
+            r = u
+        else:
+            r = jnp.where(flat < 4 * per, u, 0.0) - corner_r[g]
+        send_corners(k + groups, weights, r * corner_inv[g])
+
     def fill(g, slot, parts):
         v = jnp.concatenate(parts, axis=0)
         top = v.astype(bf16)
@@ -274,6 +381,8 @@
             base = g * per
             k = it * groups + g
             merged = arrive(k)
+            if it < ITERS - 1:
+                corner_step(it, g, k, merged)
             if it == 0 and g == 0:
                 for e in range(2):
                     save(w, modes + e, assembled(k, modes + e, per + e, merged))
@@ -480,6 +589,7 @@
             pltpu.VMEM((rounds, 2, slots, cols), f32),
             pltpu.VMEM((rounds, 2, q, LANES), f32),
             pltpu.VMEM((rounds, 2, q, LANES), f32),
+            pltpu.VMEM((rounds, 8, LANES), f32),
             pltpu.VMEM((rounds, 4, 1, LANES), f32),
             line,
             pltpu.VMEM((ny * nk * nx, 1, LANES), f32),

time: 41.4 us -> 39.9 us (0.964)
  Pallas kernels: 40.7 us -> 39.2 us
    pallas_call x1, Pallas kernels: 38.9 us -> 37.3 us  [shards(): pl.pallas_call(functools.partial(kernel, nc, ns, modes, groups), out_shap...]
where the time goes in v3:
time: 39.9 us; the launch traced here: 39.8 us
  Pallas kernels  39.2 us (98%)
  between operations  0.64 us (2%)
    pallas_call x1, Pallas kernels, shards(): pl.pallas_call(functools.partial(kernel, nc, ns, modes, groups), out_shap...  37.3 us
    pallas_call x1, Pallas kernels, shards(): pl.pallas_call(node_order, out_shape=[shape] * 2, in_specs=[vm] * 6, out_...  1.82 us

profile of v3, /device:TPU:1, one launch (start us, length us, event | category | flops | bytes accessed | tf_op | source)
XLA Modules:
  0.0 39.8 jit_solution(868548107070902790)
XLA Ops:
  0.6 37.3 %shard_map.77 = (f32[12,96,256]{2,1,0:T(8,128)S(1)}, f32[12,96,256]{2,1,0:T(8,128)S(1)}, f32[12,96,256]{2,1,0:T(8,128)S(1)}, f32[12,96,256]{2,1,0:T(8,128)S(1)},...) custom-call(f32[12]{0:T(128)} %scale_hbm.1, f32[12,96,256]{2,1,0:T(8,128)} %forcing_ref.1, f32[96,256]{1,0:T(8,128)} %metric_ref.1, ...), custom_call_target="tpu_custom_call" | custom-call | tf_op jit(solution)/shard_map/pallas_call | solution.py:575
  38.0 1.8 %shard_map.78 = (f32[12,96,256]{2,1,0:T(8,128)}, f32[12,96,256]{2,1,0:T(8,128)}) custom-call(f32[12,96,256]{2,1,0:T(8,128)S(1)} %get-tuple-element.8.r0, f32[12,96,256]{2,1,0:T(8,128)S(1)} %get-tuple-element.9.r1, f32[12,96,256]{2,1,0:T(8,128)S(1)} %get-tuple-element.10.r2, f32[12,96,256]{2,1,0:T(8,128)S(1)} %get-tuple-element.11.u2, ...), custom_call_target="tpu_custom_call" | custom-call | tf_op jit(solution)/shard_map/pallas_call | solution.py:612

commit v4 on v3

--- a/solution.py
+++ b/solution.py
@@ -350,7 +350,7 @@
         zcat[g, at, cols:] = (v - top.astype(f32)).astype(bf16)
 
     def multiply(g, table_ref):
-        gout[...] = (
+        gout[g] = (
             jnp.dot(zcat[g], table_ref[:2 * cols, :], preferred_element_type=f32)
             + jnp.dot(zcat[g, :, :cols], table_ref[2 * cols:, :], preferred_element_type=f32))
 
@@ -361,20 +361,39 @@
         line = (parts[0] + parts[3]) * 0.5 + (parts[1] + parts[2])
         return jnp.sum(jnp.where(on_edge, line * 0.5, line), axis=0, keepdims=True)
 
-    def finish(g, k, base):
+    def taken(g, slot):
+        return [gout[g, pl.ds(pl.multiple_of(slot * rows + p * q, q), q), :] for p in range(4)]
+
+    def divergence(g, k, base):
         multiply(g, div_ref)
 
         def third(slot, carry):
             m = base + slot
-            h = [u + gout[pl.ds(pl.multiple_of(slot * rows + p * q, q), q), :]
-                 for p, u in enumerate(load(w, m))]
             if k < ITERS - 1:
-                zh = [u * v for u, v in zip(load(z, m), h)]
-                sums[2 * k + 1, pl.ds(m, 1), :] = total_rows(zh)
+                own = load(w, m)
+            else:
+                fg = load(z, m)
+                zz = [u * v for u, v in zip(load(r2, m), load(invp, m))]
+                own = [t * u + combo(SLOPES[:, a], fg)
+                       for a, (t, u) in enumerate(zip(load2(mass), zz))]
+            h = [u + v for u, v in zip(own, taken(g, slot))]
             return pack((k + 1) * groups + g, m, slot, h, carry)
 
         tops = lax.fori_loop(0, per, third, (zero, zero), unroll=UNROLL)
         send((k + 1) * groups + g, tops)
+
+    def tally(it):
+        def body(m, carry):
+            rr, inv, t = load((r0, r1)[it], m), load(invp, m), load(w, m)
+            zz = [u * v for u, v in zip(rr, inv)]
+            uu = rr if it == 0 else [u + v for u, v in zip(rr, load(r0, m))]
+            sums[2 * it, pl.ds(m, 1), :] = shared_rows([u * v for u, v in zip(uu, zz)])
+            zt = [u * v for u, v in zip(zz, t)]
+            edge = jnp.where(row_at == q - 1, zt[3], 0.0)
+            sums[2 * it + 1, pl.ds(m, 1), :] = total_rows([zt[0], zt[1], zt[2], edge])
+            return carry
+
+        lax.fori_loop(0, modes, body, 0)
 
     for it in range(ITERS):
         for g in range(groups):
@@ -406,37 +425,41 @@
                     save(r2, m, rr)
                 zz = [u * v for u, v in zip(rr, inv)]
                 fill(g, slot, zz)
-                sums[2 * it, pl.ds(m, 1), :] = shared_rows([u * v for u, v in zip(uu, zz)])
                 f = load2(flux)
                 gx = [combo(SLOPES[a], zz) for a in range(4)]
                 fg = [f[a] * gx[a] * scale_ref[m] for a in range(4)]
                 mz = [u * v for u, v in zip(load2(mass), zz)]
                 if it < ITERS - 1:
-                    save(z, m, zz)
+                    save(w, m, [mz[a] + combo(SLOPES[:, a], fg) for a in range(4)])
                 else:
+                    save(z, m, fg)
+                    sums[2 * it, pl.ds(m, 1), :] = shared_rows([u * v for u, v in zip(uu, zz)])
                     sums[2 * it + 1, pl.ds(m, 1), :] = total_rows(
                         [u * v + s * t for u, v, s, t in zip(mz, zz, fg, gx)])
-                save(w, m, [mz[a] + combo(SLOPES[:, a], fg) for a in range(4)])
                 return carry
 
             lax.fori_loop(0, per, first, 0, unroll=UNROLL)
             multiply(g, grad_ref)
 
-            def second(slot, carry, it=it, g=g, base=base):
-                m = base + slot
-                grad = [gout[pl.ds(pl.multiple_of(slot * rows + p * q, q), q), :]
-                        for p in range(4)]
-                fy = [u * v * scale_ref[m] for u, v in zip(load2(flux), grad)]
-                if it == ITERS - 1:
-                    e = 2 * it + 1
-                    sums[e, pl.ds(m, 1), :] = sums[e, pl.ds(m, 1), :] + total_rows(
-                        [u * v for u, v in zip(fy, grad)])
-                fill(g, slot, fy)
+            def weigh(slot, carry, it=it, g=g, base=base):
+                grad = taken(g, slot)
+                fill(g, slot, [u * v * scale_ref[base + slot] for u, v in zip(load2(flux), grad)])
                 return carry
 
-            lax.fori_loop(0, per, second, 0, unroll=UNROLL)
+            def square(slot, carry, it=it, g=g, base=base):
+                m, e = base + slot, 2 * it + 1
+                more = [u * v * v for u, v in zip(load2(flux), taken(g, slot))]
+                sums[e, pl.ds(m, 1), :] = (
+                    sums[e, pl.ds(m, 1), :] + scale_ref[m] * total_rows(more))
+                return carry
+
             if it < ITERS - 1:
-                finish(g, it, base)
+                lax.fori_loop(0, per, weigh, 0, unroll=UNROLL)
+                divergence(g, it, base)
+            else:
+                lax.fori_loop(0, per, square, 0, unroll=UNROLL)
+        if it < ITERS - 1:
+            tally(it)
 
     high = lax.broadcasted_iota(jnp.int32, (FIELD, LANES), 0)
     wide = lax.broadcasted_iota(jnp.int32, (FIELD, LANES), 1)
@@ -462,7 +485,14 @@
 
     share(0, line, near_tx, near_rx, near)
     for g in range(groups):
-        finish(g, ITERS - 1, g * per)
+
+        def weigh(slot, carry, g=g):
+            fill(g, slot, [u * v * scale_ref[g * per + slot]
+                           for u, v in zip(load2(flux), taken(g, slot))])
+            return carry
+
+        lax.fori_loop(0, per, weigh, 0, unroll=UNROLL)
+        divergence(g, ITERS - 1, g * per)
     share(1, gather(0, near_rx), far_tx, far_rx, far)
     for g in range(groups):
         k = ITERS * groups + g
@@ -583,7 +613,7 @@
             pltpu.VMEM((rows, cols), f32),
             pltpu.VMEM((rows, cols), f32),
             pltpu.VMEM((groups, per * rows, 2 * cols), bf16),
-            pltpu.VMEM((per * rows, cols), f32),
+            pltpu.VMEM((groups, per * rows, cols), f32),
             pltpu.VMEM((PRODUCTS, FIELD, cols), f32),
             pltpu.VMEM((rounds, 2, slots, cols), f32),
             pltpu.VMEM((rounds, 2, slots, cols), f32),

time: 39.9 us -> 40.5 us (1.015)
    pallas_call x1, Pallas kernels: 37.3 us -> 37.8 us  [shards(): pl.pallas_call(functools.partial(kernel, nc, ns, modes, groups), out_shap...]
where the time goes in v4:
time: 40.5 us; the launch traced here: 40.4 us
  Pallas kernels  39.6 us (98%)
  between operations  0.8 us (2%)
    pallas_call x1, Pallas kernels, shards(): pl.pallas_call(functools.partial(kernel, nc, ns, modes, groups), out_shap...  37.8 us
    pallas_call x1, Pallas kernels, shards(): pl.pallas_call(node_order, out_shape=[shape] * 2, in_specs=[vm] * 6, out_...  1.82 us

profile of v4, /device:TPU:1, one launch (start us, length us, event | category | flops | bytes accessed | tf_op | source)
XLA Modules:
  0.0 40.4 jit_solution(7607464287568301623)
XLA Ops:
  0.6 37.8 %shard_map.77 = (f32[12,96,256]{2,1,0:T(8,128)S(1)}, f32[12,96,256]{2,1,0:T(8,128)S(1)}, f32[12,96,256]{2,1,0:T(8,128)S(1)}, f32[12,96,256]{2,1,0:T(8,128)S(1)},...) custom-call(f32[12]{0:T(128)} %scale_hbm.1, f32[12,96,256]{2,1,0:T(8,128)} %forcing_ref.1, f32[96,256]{1,0:T(8,128)} %metric_ref.1, ...), custom_call_target="tpu_custom_call" | custom-call | tf_op jit(solution)/shard_map/pallas_call | solution.py:605
  38.4 1.8 %shard_map.78 = (f32[12,96,256]{2,1,0:T(8,128)}, f32[12,96,256]{2,1,0:T(8,128)}) custom-call(f32[12,96,256]{2,1,0:T(8,128)S(1)} %get-tuple-element.8.r0, f32[12,96,256]{2,1,0:T(8,128)S(1)} %get-tuple-element.9.r1, f32[12,96,256]{2,1,0:T(8,128)S(1)} %get-tuple-element.10.r2, f32[12,96,256]{2,1,0:T(8,128)S(1)} %get-tuple-element.11.u2, ...), custom_call_target="tpu_custom_call" | custom-call | tf_op jit(solution)/shard_map/pallas_call | solution.py:642

commit v5 on v3

--- a/solution.py
+++ b/solution.py
@@ -93,21 +93,27 @@
     core, chip = lax.rem(me_c, nk), me_c // nk
     at_z, at_y = lax.rem(chip, nz), chip // nz
     subs = [me_s if dx == 0 else lax.rem(me_s + dx, nx) for dx in range(nx)]
-    near, far = [], []
-    for dy in range(ny):
-        y = at_y if dy == 0 else lax.rem(at_y + dy, ny)
-        for dk in range(nk):
-            k = core if dk == 0 else 1 - core
-            c = (y * nz + at_z) * nk + k
-            near += [(c, subs[dx]) for dx in range(nx)]
-    for dz in range(nz):
-        far.append(((at_y * nz + lax.rem(at_z + dz, nz)) * nk + core, me_s))
-    near, far = near[1:], far[1:]
+    ys = [at_y if dy == 0 else lax.rem(at_y + dy, ny) for dy in range(ny)]
+    zs = [at_z if dz == 0 else lax.rem(at_z + dz, nz) for dz in range(nz)]
+
+    def ring(step, size):
+        return min(step, size - step)
+
+    plane = sorted(
+        [(dy, dk, dx) for dy in range(ny) for dk in range(nk) for dx in range(nx)][1:],
+        key=lambda o: -(2 * ring(o[0], ny) + o[1] + 2 * ring(o[2], nx)))
+    near = [((ys[dy] * nz + at_z) * nk + (1 - core if dk else core), subs[dx])
+            for dy, dk, dx in plane]
+    line_z = sorted(range(1, nz), key=lambda dz: -ring(dz, nz))
+    far = [((at_y * nz + zs[dz]) * nk + core, me_s) for dz in line_z]
 
     barrier = pltpu.get_barrier_semaphore()
     greeted = [
-        (up, left), (up, right), (down, left), (down, right), (up, me_s), (down, me_s),
-        (me_c, left), (me_c, right)] + near + far
+        (up, left), (up, right), (down, left), (down, right)]
+    greeted += [((ys[dy] * nz + at_z) * nk + core, me_s) for dy in range(1, ny)]
+    greeted += [((at_y * nz + zs[dz]) * nk + core, me_s)
+                for dz in sorted({1, 2, nz - 1, nz - 2} - {0, nz})]
+    greeted += [(up, me_s), (down, me_s), (me_c, left), (me_c, right)]
     for where in greeted:
         pl.semaphore_signal(barrier, inc=1, device_id=where, device_id_type=MESH)
 

time: 39.9 us -> 40.3 us (1.010)
  no operation moved by 1% of the time
where the time goes in v5:
time: 40.3 us; the launch traced here: 40.2 us
  Pallas kernels  39.5 us (98%)
  between operations  0.64 us (2%)
    pallas_call x1, Pallas kernels, shards(): pl.pallas_call(functools.partial(kernel, nc, ns, modes, groups), out_shap...  37.7 us
    pallas_call x1, Pallas kernels, shards(): pl.pallas_call(node_order, out_shape=[shape] * 2, in_specs=[vm] * 6, out_...  1.82 us

profile of v5, /device:TPU:1, one launch (start us, length us, event | category | flops | bytes accessed | tf_op | source)
XLA Modules:
  0.0 40.2 jit_solution(13094636063702575298)
XLA Ops:
  0.6 37.7 %shard_map.77 = (f32[12,96,256]{2,1,0:T(8,128)S(1)}, f32[12,96,256]{2,1,0:T(8,128)S(1)}, f32[12,96,256]{2,1,0:T(8,128)S(1)}, f32[12,96,256]{2,1,0:T(8,128)S(1)},...) custom-call(f32[12]{0:T(128)} %scale_hbm.1, f32[12,96,256]{2,1,0:T(8,128)} %forcing_ref.1, f32[96,256]{1,0:T(8,128)} %metric_ref.1, ...), custom_call_target="tpu_custom_call" | custom-call | tf_op jit(solution)/shard_map/pallas_call | solution.py:581
  38.3 1.8 %shard_map.78 = (f32[12,96,256]{2,1,0:T(8,128)}, f32[12,96,256]{2,1,0:T(8,128)}) custom-call(f32[12,96,256]{2,1,0:T(8,128)S(1)} %get-tuple-element.8.r0, f32[12,96,256]{2,1,0:T(8,128)S(1)} %get-tuple-element.9.r1, f32[12,96,256]{2,1,0:T(8,128)S(1)} %get-tuple-element.10.r2, f32[12,96,256]{2,1,0:T(8,128)S(1)} %get-tuple-element.11.u2, ...), custom_call_target="tpu_custom_call" | custom-call | tf_op jit(solution)/shard_map/pallas_call | solution.py:618

commit v6 on v5

--- a/solution.py
+++ b/solution.py
@@ -55,13 +55,17 @@
     return nc // (2 * depth), depth, 2, ns
 
 
+def landed(ref, sem):
+    pltpu.make_async_copy(ref, ref, sem).wait()
+
+
 def kernel(
     nc, ns, modes, groups,
     scale_hbm, forcing_ref, metric_ref, jac_ref, grad_hbm, div_hbm,
     r0, r1, r2, u2, invp, coef,
     z, w, mass, flux, zcat, gout, sums,
     row_tx, row_rx, col_tx, col_rx, cor_tx, cor_rx, near_tx, near_rx, far_tx, far_rx,
-    source, factors, grad_ref, div_ref, scale_ref,
+    source, factors, gauge, grad_ref, div_ref, scale_ref,
     htx_sem, hrx_sem, atx_sem, arx_sem, in_sem, table_sem,
 ):
     rows, cols = metric_ref.shape
@@ -74,11 +78,11 @@
     for c in range(tiles):
         cut = pl.ds(c * LANES, LANES)
         loads += [
-            pltpu.make_async_copy(jac_ref.at[:, cut], factors.at[0, c], in_sem.at[0, c]),
-            pltpu.make_async_copy(metric_ref.at[:, cut], factors.at[1, c], in_sem.at[1, c]),
+            pltpu.make_async_copy(jac_ref.at[:, cut], factors.at[0, c], in_sem.at[0]),
+            pltpu.make_async_copy(metric_ref.at[:, cut], factors.at[1, c], in_sem.at[0]),
         ]
         sources.append(
-            pltpu.make_async_copy(forcing_ref.at[:, :, cut], source.at[c], in_sem.at[2, c]))
+            pltpu.make_async_copy(forcing_ref.at[:, :, cut], source.at[c], in_sem.at[1]))
     div_load = pltpu.make_async_copy(div_hbm, div_ref, table_sem.at[0])
     grad_load = pltpu.make_async_copy(grad_hbm, grad_ref, table_sem.at[1])
     scale_load = pltpu.make_async_copy(scale_hbm, scale_ref, table_sem.at[2])
@@ -169,9 +173,9 @@
         ]
         return [
             pltpu.make_async_remote_copy(
-                src_ref=src, dst_ref=dst, send_sem=htx_sem.at[k, e], recv_sem=hrx_sem.at[k, e],
+                src_ref=src, dst_ref=dst, send_sem=htx_sem.at[k], recv_sem=hrx_sem.at[k],
                 device_id=where, device_id_type=MESH)
-            for e, (src, dst, where) in enumerate(plan)
+            for src, dst, where in plan
         ]
 
     def send(k, tops):
@@ -180,8 +184,7 @@
             copy.start()
 
     def arrive(k):
-        for copy in halo_copies(k):
-            copy.wait_recv()
+        landed(gauge, hrx_sem.at[k])
         ph = lax.broadcasted_iota(jnp.int32, (1, LANES), 1) % 4
         edge_row = lax.broadcasted_iota(jnp.int32, (q, LANES), 0)
         merged = []
@@ -215,8 +218,7 @@
     edge_w, mid_w = f32(1.0 / 6.0), f32(5.0 / 6.0)
     col_w = jnp.where(on_edge, edge_w, mid_w)
     mw, fw = [], []
-    for copy in loads:
-        copy.wait()
+    landed(factors, in_sem.at[0])
     for p in range(4):
         grid_w = col_w * (edge_w if p in (0, 3) else mid_w)
         mw.append(strided([factors.at[0, c] for c in range(tiles)], p, q) * grid_w)
@@ -232,8 +234,7 @@
     squared = SLOPES * SLOPES
     lap = [combo(squared[:, a], fw) + by_cols[a * q:(a + 1) * q, :] for a in range(4)]
     tops = pack(0, modes + 1, per + 1, lap, tops)
-    for copy in sources:
-        copy.wait()
+    landed(source, in_sem.at[1])
     for g in range(groups):
 
         def start_body(slot, carry, g=g):
@@ -462,8 +463,7 @@
                 recv_sem=arx_sem.at[stage], device_id=where, device_id_type=MESH).start()
 
     def gather(stage, rx):
-        got = rx.at[pl.ds(1, rx.shape[0] - 1)]
-        pltpu.make_async_copy(got, got, arx_sem.at[stage]).wait()
+        landed(rx.at[pl.ds(1, rx.shape[0] - 1)], arx_sem.at[stage])
         return jnp.sum(rx[...], axis=0)
 
     share(0, line, near_tx, near_rx, near)
@@ -509,11 +509,9 @@
         coef[e] = c
 
     for k in range((ITERS + 1) * groups):
-        for copy in halo_copies(k):
-            copy.wait_send()
+        landed(gauge, htx_sem.at[k])
     for stage, rx in enumerate((near_rx, far_rx)):
-        sent = rx.at[pl.ds(1, rx.shape[0] - 1)]
-        pltpu.make_async_copy(sent, sent, atx_sem.at[stage]).wait()
+        landed(rx.at[pl.ds(1, rx.shape[0] - 1)], atx_sem.at[stage])
 
 
 def node_order(r0, r1, r2, u2, invp, coef, sol_ref, res_ref, sol_buf, res_buf, sem):
@@ -603,13 +601,14 @@
             pltpu.VMEM((nz, 1, LANES), f32),
             split,
             pltpu.VMEM((2, tiles, rows, LANES), f32),
+            pltpu.VMEM((4 + 2 * slots * tiles + 2 * q, LANES), f32),
             table, table,
             pltpu.SMEM((modes,), f32),
-            pltpu.SemaphoreType.DMA((rounds, 8)),
-            pltpu.SemaphoreType.DMA((rounds, 8)),
+            pltpu.SemaphoreType.DMA((rounds,)),
+            pltpu.SemaphoreType.DMA((rounds,)),
             pltpu.SemaphoreType.DMA((2,)),
             pltpu.SemaphoreType.DMA((2,)),
-            pltpu.SemaphoreType.DMA((3, tiles)),
+            pltpu.SemaphoreType.DMA((2,)),
             pltpu.SemaphoreType.DMA((3,)),
         ],
         compiler_params=pltpu.CompilerParams(

time: 40.3 us -> 39.1 us (0.970)
  Pallas kernels: 39.5 us -> 38.4 us
    pallas_call x1, Pallas kernels: 37.7 us -> 36.6 us  [shards(): pl.pallas_call(functools.partial(kernel, nc, ns, modes, groups), out_shap...]
where the time goes in v6:
time: 39.1 us; the launch traced here: 39 us
  Pallas kernels  38.4 us (98%)
  between operations  0.64 us (2%)
    pallas_call x1, Pallas kernels, shards(): pl.pallas_call(functools.partial(kernel, nc, ns, modes, groups), out_shap...  36.6 us
    pallas_call x1, Pallas kernels, shards(): pl.pallas_call(node_order, out_shape=[shape] * 2, in_specs=[vm] * 6, out_...  1.82 us

profile of v6, /device:TPU:1, one launch (start us, length us, event | category | flops | bytes accessed | tf_op | source)
XLA Modules:
  0.0 39.0 jit_solution(15034057093030626953)
XLA Ops:
  0.6 36.6 %shard_map.77 = (f32[12,96,256]{2,1,0:T(8,128)S(1)}, f32[12,96,256]{2,1,0:T(8,128)S(1)}, f32[12,96,256]{2,1,0:T(8,128)S(1)}, f32[12,96,256]{2,1,0:T(8,128)S(1)},...) custom-call(f32[12]{0:T(128)} %scale_hbm.1, f32[12,96,256]{2,1,0:T(8,128)} %forcing_ref.1, f32[96,256]{1,0:T(8,128)} %metric_ref.1, ...), custom_call_target="tpu_custom_call" | custom-call | tf_op jit(solution)/shard_map/pallas_call | solution.py:579
  37.2 1.8 %shard_map.78 = (f32[12,96,256]{2,1,0:T(8,128)}, f32[12,96,256]{2,1,0:T(8,128)}) custom-call(f32[12,96,256]{2,1,0:T(8,128)S(1)} %get-tuple-element.8.r0, f32[12,96,256]{2,1,0:T(8,128)S(1)} %get-tuple-element.9.r1, f32[12,96,256]{2,1,0:T(8,128)S(1)} %get-tuple-element.10.r2, f32[12,96,256]{2,1,0:T(8,128)S(1)} %get-tuple-element.11.u2, ...), custom_call_target="tpu_custom_call" | custom-call | tf_op jit(solution)/shard_map/pallas_call | solution.py:617

commit v7 on v6

--- a/solution.py
+++ b/solution.py
@@ -53,6 +53,27 @@
 def planes(nc, ns):
     depth = 8 if nc % 16 == 0 else 2
     return nc // (2 * depth), depth, 2, ns
+
+
+def slope(z):
+    even = (z[1] + z[2]) - (z[0] + z[3])
+    outer, inner = z[3] - z[0], z[2] - z[1]
+    half = 0.5 * (SLOPES[:, ::-1] - SLOPES)
+    a = outer * f32(half[0, 0]) + inner * f32(half[0, 1])
+    b = outer * f32(half[1, 0]) + inner * f32(half[1, 1])
+    e0 = even * f32(0.5 * (SLOPES[0, 1] + SLOPES[0, 2]))
+    e1 = even * f32(0.5 * (SLOPES[1, 1] + SLOPES[1, 2]))
+    return [a + e0, b + e1, b - e1, a - e0]
+
+
+def fall(f):
+    s0, s1, d0, d1 = f[0] + f[3], f[1] + f[2], f[3] - f[0], f[2] - f[1]
+    even = 0.5 * (SLOPES[:, 1] + SLOPES[:, 2])
+    half = 0.5 * (SLOPES[:, ::-1] - SLOPES)
+    x = d0 * f32(even[0]) + d1 * f32(even[1])
+    y = s0 * f32(half[0, 0]) + s1 * f32(half[1, 0])
+    v = s0 * f32(half[0, 1]) + s1 * f32(half[1, 1])
+    return [x - y, (0.0 - x) - v, v - x, x + y]
 
 
 def landed(ref, sem):
@@ -197,18 +218,39 @@
             merged.append(c)
         return merged
 
-    def assembled(k, m, slot, merged):
-        t = load(w, m)
-        t[0] = t[0] + jnp.where(row_at == 0, row_rx[k, 0, pl.ds(slot, 1), :], 0.0)
-        t[3] = t[3] + jnp.where(row_at == q - 1, row_rx[k, 1, pl.ds(slot, 1), :], 0.0)
+    few_rows = lax.broadcasted_iota(jnp.int32, (8, cols), 0)
+    few_at = lax.broadcasted_iota(jnp.int32, (8, cols), 1)
+    few_lane = lax.broadcasted_iota(jnp.int32, (8, LANES), 1)
+    few_next = (few_at % 4 == 3) & (few_at != cols - 1)
+    few_prev = (few_at % 4 == 0) & (few_at != 0)
+    few_edge = (few_at % 4 == 3) | (few_at % 4 == 0)
+    chunks = q // 8
+
+    def chunk(ref, m, n):
+        return [ref[m, p * q + 8 * n:p * q + 8 * n + 8, :] for p in range(4)]
+
+    def chunk2(ref, n):
+        return [ref[p * q + 8 * n:p * q + 8 * n + 8, :] for p in range(4)]
+
+    def keep(ref, m, n, parts):
+        for p in range(4):
+            ref[m, p * q + 8 * n:p * q + 8 * n + 8, :] = parts[p]
+
+    def joined(k, m, slot, merged, n):
+        t = chunk(w, m, n)
+        if n == 0:
+            t[0] = t[0] + jnp.where(few_rows == 0, row_rx[k, 0, pl.ds(slot, 1), :], 0.0)
+        if n == chunks - 1:
+            t[3] = t[3] + jnp.where(few_rows == 7, row_rx[k, 1, pl.ds(slot, 1), :], 0.0)
+        near_side, far_side = [v[8 * n:8 * n + 8] for v in merged]
         out = []
         for p in range(4):
             at = 4 * slot + p
             c = t[p] + jnp.where(
-                take_next, pltpu.roll(t[p], cols - 1, 1),
-                jnp.where(take_prev, pltpu.roll(t[p], 1, 1), 0.0))
-            a = jnp.where(lane == 0, pltpu.roll(merged[0], LANES - at, 1), 0.0)
-            b = jnp.where(lane == LANES - 1, pltpu.roll(merged[1], LANES - 1 - at, 1), 0.0)
+                few_next, pltpu.roll(t[p], cols - 1, 1),
+                jnp.where(few_prev, pltpu.roll(t[p], 1, 1), 0.0))
+            a = jnp.where(few_lane == 0, pltpu.roll(near_side, LANES - at, 1), 0.0)
+            b = jnp.where(few_lane == LANES - 1, pltpu.roll(far_side, LANES - 1 - at, 1), 0.0)
             pieces = [c[:, e * LANES:(e + 1) * LANES] for e in range(tiles)]
             pieces[0] = pieces[0] + a
             pieces[-1] = pieces[-1] + b
@@ -349,35 +391,47 @@
             r = jnp.where(flat < 4 * per, u, 0.0) - corner_r[g]
         send_corners(k + groups, weights, r * corner_inv[g])
 
-    def fill(g, slot, parts):
+    def fill(g, slot, n, parts):
         v = jnp.concatenate(parts, axis=0)
         top = v.astype(bf16)
-        at = pl.ds(pl.multiple_of(slot * rows, rows), rows)
+        at = pl.ds(pl.multiple_of(slot * rows + 32 * n, 32), 32)
         zcat[g, at, :cols] = top
         zcat[g, at, cols:] = (v - top.astype(f32)).astype(bf16)
+
+    def taken(slot, n):
+        return [gout[pl.ds(pl.multiple_of(slot * rows + 32 * n + 8 * p, 8), 8), :]
+                for p in range(4)]
 
     def multiply(g, table_ref):
         gout[...] = (
             jnp.dot(zcat[g], table_ref[:2 * cols, :], preferred_element_type=f32)
             + jnp.dot(zcat[g, :, :cols], table_ref[2 * cols:, :], preferred_element_type=f32))
 
-    def total_rows(parts):
-        return jnp.sum((parts[0] + parts[3]) + (parts[1] + parts[2]), axis=0, keepdims=True)
-
-    def shared_rows(parts):
-        line = (parts[0] + parts[3]) * 0.5 + (parts[1] + parts[2])
-        return jnp.sum(jnp.where(on_edge, line * 0.5, line), axis=0, keepdims=True)
+    def total(parts):
+        return (parts[0] + parts[3]) + (parts[1] + parts[2])
+
+    def shared(parts):
+        return (parts[0] + parts[3]) * 0.5 + (parts[1] + parts[2])
+
+    def put(e, m, line):
+        sums[e, pl.ds(m, 1), :] = jnp.sum(line, axis=0, keepdims=True)
 
     def finish(g, k, base):
         multiply(g, div_ref)
 
         def third(slot, carry):
             m = base + slot
-            h = [u + gout[pl.ds(pl.multiple_of(slot * rows + p * q, q), q), :]
-                 for p, u in enumerate(load(w, m))]
+            h, line = [], 0.0
+            for n in range(chunks):
+                zz = chunk(z, m, n)
+                part = [t * u + scale_ref[m] * (v + s) for t, u, v, s in zip(
+                    chunk2(mass, n), zz, chunk(w, m, n), taken(slot, n))]
+                if k < ITERS - 1:
+                    line = line + total([u * v for u, v in zip(zz, part)])
+                h.append(part)
             if k < ITERS - 1:
-                zh = [u * v for u, v in zip(load(z, m), h)]
-                sums[2 * k + 1, pl.ds(m, 1), :] = total_rows(zh)
+                put(2 * k + 1, m, line)
+            h = [jnp.concatenate([part[p] for part in h], axis=0) for p in range(4)]
             return pack((k + 1) * groups + g, m, slot, h, carry)
 
         tops = lax.fori_loop(0, per, third, (zero, zero), unroll=UNROLL)
@@ -392,53 +446,58 @@
                 corner_step(it, g, k, merged)
             if it == 0 and g == 0:
                 for e in range(2):
-                    save(w, modes + e, assembled(k, modes + e, per + e, merged))
+                    got = [joined(k, modes + e, per + e, merged, n) for n in range(chunks)]
+                    for n in range(chunks):
+                        keep(w, modes + e, n, got[n])
 
             def first(slot, carry, it=it, g=g, k=k, base=base, merged=merged):
                 m = base + slot
-                uu = assembled(k, m, slot, merged)
-                if it == 0:
-                    rr = uu
-                    inv = [1.0 / (u + scale_ref[m] * v)
-                           for u, v in zip(load(w, modes), load(w, modes + 1))]
-                    save(invp, m, inv)
-                    save(r0, m, rr)
-                elif it == 1:
-                    rr = [u - v for u, v in zip(uu, load(r0, m))]
-                    inv = load(invp, m)
-                    save(r1, m, rr)
-                else:
-                    rr = [2.0 * (u - v) - s for u, v, s in zip(uu, load(r1, m), load(r0, m))]
-                    inv = load(invp, m)
-                    save(r2, m, rr)
-                zz = [u * v for u, v in zip(rr, inv)]
-                fill(g, slot, zz)
-                sums[2 * it, pl.ds(m, 1), :] = shared_rows([u * v for u, v in zip(uu, zz)])
-                f = load2(flux)
-                gx = [combo(SLOPES[a], zz) for a in range(4)]
-                fg = [f[a] * gx[a] * scale_ref[m] for a in range(4)]
-                mz = [u * v for u, v in zip(load2(mass), zz)]
-                if it < ITERS - 1:
-                    save(z, m, zz)
-                else:
-                    sums[2 * it + 1, pl.ds(m, 1), :] = total_rows(
-                        [u * v + s * t for u, v, s, t in zip(mz, zz, fg, gx)])
-                save(w, m, [mz[a] + combo(SLOPES[:, a], fg) for a in range(4)])
+                line, energy = 0.0, 0.0
+                for n in range(chunks):
+                    uu = joined(k, m, slot, merged, n)
+                    if it == 0:
+                        rr = uu
+                        inv = [1.0 / (u + scale_ref[m] * v)
+                               for u, v in zip(chunk(w, modes, n), chunk(w, modes + 1, n))]
+                        keep(invp, m, n, inv)
+                    elif it == 1:
+                        rr = [u - v for u, v in zip(uu, chunk(r0, m, n))]
+                        inv = chunk(invp, m, n)
+                    else:
+                        rr = [2.0 * (u - v) - s for u, v, s in zip(
+                            uu, chunk(r1, m, n), chunk(r0, m, n))]
+                        inv = chunk(invp, m, n)
+                    keep((r0, r1, r2)[it], m, n, rr)
+                    zz = [u * v for u, v in zip(rr, inv)]
+                    keep(z, m, n, zz)
+                    fill(g, slot, n, zz)
+                    line = line + shared([u * v for u, v in zip(uu, zz)])
+                    gx = slope(zz)
+                    fg = [u * v for u, v in zip(chunk2(flux, n), gx)]
+                    keep(w, m, n, fall(fg))
+                    if it == ITERS - 1:
+                        energy = energy + (
+                            total([t * u * u for t, u in zip(chunk2(mass, n), zz)])
+                            + scale_ref[m] * total([u * v for u, v in zip(fg, gx)]))
+                put(2 * it, m, jnp.where(few_edge, line * 0.5, line))
+                if it == ITERS - 1:
+                    put(2 * it + 1, m, energy)
                 return carry
 
             lax.fori_loop(0, per, first, 0, unroll=UNROLL)
             multiply(g, grad_ref)
 
             def second(slot, carry, it=it, g=g, base=base):
-                m = base + slot
-                grad = [gout[pl.ds(pl.multiple_of(slot * rows + p * q, q), q), :]
-                        for p in range(4)]
-                fy = [u * v * scale_ref[m] for u, v in zip(load2(flux), grad)]
+                m, e, line = base + slot, 2 * it + 1, 0.0
+                for n in range(chunks):
+                    grad = taken(slot, n)
+                    fy = [u * v for u, v in zip(chunk2(flux, n), grad)]
+                    if it == ITERS - 1:
+                        line = line + total([u * v for u, v in zip(fy, grad)])
+                    fill(g, slot, n, fy)
                 if it == ITERS - 1:
-                    e = 2 * it + 1
-                    sums[e, pl.ds(m, 1), :] = sums[e, pl.ds(m, 1), :] + total_rows(
-                        [u * v for u, v in zip(fy, grad)])
-                fill(g, slot, fy)
+                    sums[e, pl.ds(m, 1), :] = sums[e, pl.ds(m, 1), :] + scale_ref[m] * jnp.sum(
+                        line, axis=0, keepdims=True)
                 return carry
 
             lax.fori_loop(0, per, second, 0, unroll=UNROLL)
@@ -476,7 +535,8 @@
 
         def last(slot, carry, g=g, k=k, merged=merged):
             m = g * per + slot
-            save(u2, m, assembled(k, m, slot, merged))
+            for n in range(chunks):
+                keep(u2, m, n, joined(k, m, slot, merged, n))
             return carry
 
         lax.fori_loop(0, per, last, 0, unroll=UNROLL)

time: 39.1 us -> 39.1 us (level)
  no operation moved by 1% of the time
where the time goes in v7:
time: 39.1 us; the launch traced here: 38.9 us
  Pallas kernels  38.3 us (98%)
  between operations  0.64 us (2%)
    pallas_call x1, Pallas kernels, shards(): pl.pallas_call(functools.partial(kernel, nc, ns, modes, groups), out_shap...  36.5 us
    pallas_call x1, Pallas kernels, shards(): pl.pallas_call(node_order, out_shape=[shape] * 2, in_specs=[vm] * 6, out_...  1.82 us

profile of v7, /device:TPU:1, one launch (start us, length us, event | category | flops | bytes accessed | tf_op | source)
XLA Modules:
  0.0 38.9 jit_solution(11100951001848155715)
XLA Ops:
  0.6 36.5 %shard_map.77 = (f32[12,96,256]{2,1,0:T(8,128)S(1)}, f32[12,96,256]{2,1,0:T(8,128)S(1)}, f32[12,96,256]{2,1,0:T(8,128)S(1)}, f32[12,96,256]{2,1,0:T(8,128)S(1)},...) custom-call(f32[12]{0:T(128)} %scale_hbm.1, f32[12,96,256]{2,1,0:T(8,128)} %forcing_ref.1, f32[96,256]{1,0:T(8,128)} %metric_ref.1, ...), custom_call_target="tpu_custom_call" | custom-call | tf_op jit(solution)/shard_map/pallas_call | solution.py:639
  37.1 1.8 %shard_map.78 = (f32[12,96,256]{2,1,0:T(8,128)}, f32[12,96,256]{2,1,0:T(8,128)}) custom-call(f32[12,96,256]{2,1,0:T(8,128)S(1)} %get-tuple-element.8.r0, f32[12,96,256]{2,1,0:T(8,128)S(1)} %get-tuple-element.9.r1, f32[12,96,256]{2,1,0:T(8,128)S(1)} %get-tuple-element.10.r2, f32[12,96,256]{2,1,0:T(8,128)S(1)} %get-tuple-element.11.u2, ...), custom_call_target="tpu_custom_call" | custom-call | tf_op jit(solution)/shard_map/pallas_call | solution.py:677

commit v8 on v7

--- a/solution.py
+++ b/solution.py
@@ -87,7 +87,7 @@
     z, w, mass, flux, zcat, gout, sums,
     row_tx, row_rx, col_tx, col_rx, cor_tx, cor_rx, near_tx, near_rx, far_tx, far_rx,
     source, factors, gauge, grad_ref, div_ref, scale_ref,
-    htx_sem, hrx_sem, atx_sem, arx_sem, in_sem, table_sem,
+    htx_sem, hrx_sem, crx_sem, atx_sem, arx_sem, in_sem, table_sem,
 ):
     rows, cols = metric_ref.shape
     q = rows // 4
@@ -194,9 +194,10 @@
         ]
         return [
             pltpu.make_async_remote_copy(
-                src_ref=src, dst_ref=dst, send_sem=htx_sem.at[k], recv_sem=hrx_sem.at[k],
+                src_ref=src, dst_ref=dst, send_sem=htx_sem.at[k],
+                recv_sem=crx_sem.at[k] if k < groups and e < 4 else hrx_sem.at[k],
                 device_id=where, device_id_type=MESH)
-            for src, dst, where in plan
+            for e, (src, dst, where) in enumerate(plan)
         ]
 
     def send(k, tops):
@@ -205,7 +206,10 @@
             copy.start()
 
     def arrive(k):
-        landed(gauge, hrx_sem.at[k])
+        if k < groups:
+            landed(gauge.at[pl.ds(0, 4)], crx_sem.at[k])
+        else:
+            landed(gauge, hrx_sem.at[k])
         ph = lax.broadcasted_iota(jnp.int32, (1, LANES), 1) % 4
         edge_row = lax.broadcasted_iota(jnp.int32, (q, LANES), 0)
         merged = []
@@ -353,7 +357,7 @@
                 lines += [col, rows_here[side]]
         return jnp.concatenate(lines, axis=0)
 
-    def send_corners(k, weights, v):
+    def set_corners(k, weights, v):
         h = weights * v
         fore = h + pltpu.roll(h, LANES - 1, 1)
         fore = fore + pltpu.roll(fore, LANES - 2, 1)
@@ -361,8 +365,6 @@
         back = back + pltpu.roll(back, 2, 1)
         h = jnp.where(low_half, fore, back)
         cor_tx[k] = h + pltpu.roll(h, slots - 1, 0)
-        for copy in halo_copies(k)[:4]:
-            copy.start()
 
     def repeat(x, slot):
         x = jnp.where(flat // 4 == slot, x, 0.0)
@@ -389,7 +391,7 @@
             r = u
         else:
             r = jnp.where(flat < 4 * per, u, 0.0) - corner_r[g]
-        send_corners(k + groups, weights, r * corner_inv[g])
+        set_corners(k + groups, weights, r * corner_inv[g])
 
     def fill(g, slot, n, parts):
         v = jnp.concatenate(parts, axis=0)
@@ -437,6 +439,29 @@
         tops = lax.fori_loop(0, per, third, (zero, zero), unroll=UNROLL)
         send((k + 1) * groups + g, tops)
 
+    def patched(k, slot, n, parts):
+        parts = list(parts)
+        for at_n, p, row, lines, at in (
+                (0, 0, 0, (0, 1), 4 * slot + 3), (chunks - 1, 3, 7, (2, 3), 4 * slot)):
+            if n != at_n:
+                continue
+            a = pltpu.roll(cor_rx[k, lines[0]], LANES - at, 1)
+            b = pltpu.roll(cor_rx[k, lines[1]], LANES - 1 - at, 1)
+            here = few_rows[:, :LANES] == row
+            pieces = [parts[p][:, e * LANES:(e + 1) * LANES] for e in range(tiles)]
+            pieces[0] = pieces[0] + jnp.where(here & (few_lane == 0), a, 0.0)
+            pieces[-1] = pieces[-1] + jnp.where(here & (few_lane == LANES - 1), b, 0.0)
+            parts[p] = jnp.concatenate(pieces, axis=1)
+        return parts
+
+    for g in range(groups):
+        landed(gauge.at[pl.ds(0, gauge.shape[0] - 4)], hrx_sem.at[g])
+        sides = [col_rx[g, 0], col_rx[g, 1]]
+        pairs = [(modes, per), (modes + 1, per + 1)] if g == 0 else []
+        for m, slot in pairs + [(g * per + e, e) for e in range(per)]:
+            for n in range(chunks):
+                keep(w, m, n, joined(g, m, slot, sides, n))
+
     for it in range(ITERS):
         for g in range(groups):
             base = g * per
@@ -446,15 +471,17 @@
                 corner_step(it, g, k, merged)
             if it == 0 and g == 0:
                 for e in range(2):
-                    got = [joined(k, modes + e, per + e, merged, n) for n in range(chunks)]
-                    for n in range(chunks):
-                        keep(w, modes + e, n, got[n])
+                    for n in (0, chunks - 1):
+                        keep(w, modes + e, n, patched(k, per + e, n, chunk(w, modes + e, n)))
 
             def first(slot, carry, it=it, g=g, k=k, base=base, merged=merged):
                 m = base + slot
                 line, energy = 0.0, 0.0
                 for n in range(chunks):
-                    uu = joined(k, m, slot, merged, n)
+                    if it == 0:
+                        uu = patched(k, slot, n, chunk(w, m, n))
+                    else:
+                        uu = joined(k, m, slot, merged, n)
                     if it == 0:
                         rr = uu
                         inv = [1.0 / (u + scale_ref[m] * v)
@@ -484,6 +511,9 @@
                     put(2 * it + 1, m, energy)
                 return carry
 
+            if it < ITERS - 1:
+                for copy in halo_copies(k + groups)[:4]:
+                    copy.start()
             lax.fori_loop(0, per, first, 0, unroll=UNROLL)
             multiply(g, grad_ref)
 
@@ -666,6 +696,7 @@
             pltpu.SMEM((modes,), f32),
             pltpu.SemaphoreType.DMA((rounds,)),
             pltpu.SemaphoreType.DMA((rounds,)),
+            pltpu.SemaphoreType.DMA((groups,)),
             pltpu.SemaphoreType.DMA((2,)),
             pltpu.SemaphoreType.DMA((2,)),
             pltpu.SemaphoreType.DMA((2,)),

time: 39.1 us -> 38.9 us (level)
  no operation moved by 1% of the time
where the time goes in v8:
time: 38.9 us; the launch traced here: 38.8 us
  Pallas kernels  38.1 us (98%)
  between operations  0.64 us (2%)
    pallas_call x1, Pallas kernels, shards(): pl.pallas_call(functools.partial(kernel, nc, ns, modes, groups), out_shap...  36.3 us
    pallas_call x1, Pallas kernels, shards(): pl.pallas_call(node_order, out_shape=[shape] * 2, in_specs=[vm] * 6, out_...  1.82 us

profile of v8, /device:TPU:1, one launch (start us, length us, event | category | flops | bytes accessed | tf_op | source)
XLA Modules:
  0.0 38.8 jit_solution(9899851815593001123)
XLA Ops:
  0.6 36.3 %shard_map.77 = (f32[12,96,256]{2,1,0:T(8,128)S(1)}, f32[12,96,256]{2,1,0:T(8,128)S(1)}, f32[12,96,256]{2,1,0:T(8,128)S(1)}, f32[12,96,256]{2,1,0:T(8,128)S(1)},...) custom-call(f32[12]{0:T(128)} %scale_hbm.1, f32[12,96,256]{2,1,0:T(8,128)} %forcing_ref.1, f32[96,256]{1,0:T(8,128)} %metric_ref.1, ...), custom_call_target="tpu_custom_call" | custom-call | tf_op jit(solution)/shard_map/pallas_call | solution.py:669
  37.0 1.8 %shard_map.78 = (f32[12,96,256]{2,1,0:T(8,128)}, f32[12,96,256]{2,1,0:T(8,128)}) custom-call(f32[12,96,256]{2,1,0:T(8,128)S(1)} %get-tuple-element.8.r0, f32[12,96,256]{2,1,0:T(8,128)S(1)} %get-tuple-element.9.r1, f32[12,96,256]{2,1,0:T(8,128)S(1)} %get-tuple-element.10.r2, f32[12,96,256]{2,1,0:T(8,128)S(1)} %get-tuple-element.11.u2, ...), custom_call_target="tpu_custom_call" | custom-call | tf_op jit(solution)/shard_map/pallas_call | solution.py:708

commit v9 on v8

--- a/solution.py
+++ b/solution.py
@@ -404,10 +404,18 @@
         return [gout[pl.ds(pl.multiple_of(slot * rows + 32 * n + 8 * p, 8), 8), :]
                 for p in range(4)]
 
-    def multiply(g, table_ref):
-        gout[...] = (
-            jnp.dot(zcat[g], table_ref[:2 * cols, :], preferred_element_type=f32)
-            + jnp.dot(zcat[g, :, :cols], table_ref[2 * cols:, :], preferred_element_type=f32))
+    def multiply(g, table_ref, part):
+        lo, hi = part[0] * rows, part[1] * rows
+        gout[lo:hi] = (
+            jnp.dot(zcat[g, lo:hi, :], table_ref[:2 * cols, :], preferred_element_type=f32)
+            + jnp.dot(zcat[g, lo:hi, :cols], table_ref[2 * cols:, :],
+                      preferred_element_type=f32))
+
+    cut = (per + 1) // 2
+    parts_of = [(0, cut), (cut, per)]
+
+    def over(part, body, carry=0):
+        return lax.fori_loop(part[0], part[1], body, carry, unroll=UNROLL)
 
     def total(parts):
         return (parts[0] + parts[3]) + (parts[1] + parts[2])
@@ -419,8 +427,6 @@
         sums[e, pl.ds(m, 1), :] = jnp.sum(line, axis=0, keepdims=True)
 
     def finish(g, k, base):
-        multiply(g, div_ref)
-
         def third(slot, carry):
             m = base + slot
             h, line = [], 0.0
@@ -436,8 +442,7 @@
             h = [jnp.concatenate([part[p] for part in h], axis=0) for p in range(4)]
             return pack((k + 1) * groups + g, m, slot, h, carry)
 
-        tops = lax.fori_loop(0, per, third, (zero, zero), unroll=UNROLL)
-        send((k + 1) * groups + g, tops)
+        return third
 
     def patched(k, slot, n, parts):
         parts = list(parts)
@@ -514,9 +519,6 @@
             if it < ITERS - 1:
                 for copy in halo_copies(k + groups)[:4]:
                     copy.start()
-            lax.fori_loop(0, per, first, 0, unroll=UNROLL)
-            multiply(g, grad_ref)
-
             def second(slot, carry, it=it, g=g, base=base):
                 m, e, line = base + slot, 2 * it + 1, 0.0
                 for n in range(chunks):
@@ -530,9 +532,21 @@
                         line, axis=0, keepdims=True)
                 return carry
 
-            lax.fori_loop(0, per, second, 0, unroll=UNROLL)
+            one, two = parts_of
+            over(one, first)
+            multiply(g, grad_ref, one)
+            over(two, first)
+            over(one, second)
+            multiply(g, grad_ref, two)
             if it < ITERS - 1:
-                finish(g, it, base)
+                third = finish(g, it, base)
+                multiply(g, div_ref, one)
+                over(two, second)
+                tops = over(one, third, (zero, zero))
+                multiply(g, div_ref, two)
+                send(k + groups, over(two, third, tops))
+            else:
+                over(two, second)
 
     high = lax.broadcasted_iota(jnp.int32, (FIELD, LANES), 0)
     wide = lax.broadcasted_iota(jnp.int32, (FIELD, LANES), 1)
@@ -557,7 +571,11 @@
 
     share(0, line, near_tx, near_rx, near)
     for g in range(groups):
-        finish(g, ITERS - 1, g * per)
+        third = finish(g, ITERS - 1, g * per)
+        multiply(g, div_ref, one)
+        tops = over(one, third, (zero, zero))
+        multiply(g, div_ref, two)
+        send(ITERS * groups + g, over(two, third, tops))
     share(1, gather(0, near_rx), far_tx, far_rx, far)
     for g in range(groups):
         k = ITERS * groups + g

time: 38.9 us -> 38.4 us (0.987)
  Pallas kernels: 38.1 us -> 37.7 us
    pallas_call x1, Pallas kernels: 36.3 us -> 35.8 us  [shards(): pl.pallas_call(functools.partial(kernel, nc, ns, modes, groups), out_shap...]
where the time goes in v9:
time: 38.4 us; the launch traced here: 38.3 us
  Pallas kernels  37.7 us (98%)
  between operations  0.64 us (2%)
    pallas_call x1, Pallas kernels, shards(): pl.pallas_call(functools.partial(kernel, nc, ns, modes, groups), out_shap...  35.8 us
    pallas_call x1, Pallas kernels, shards(): pl.pallas_call(node_order, out_shape=[shape] * 2, in_specs=[vm] * 6, out_...  1.82 us

profile of v9, /device:TPU:1, one launch (start us, length us, event | category | flops | bytes accessed | tf_op | source)
XLA Modules:
  0.0 38.3 jit_solution(2274632266554312550)
XLA Ops:
  0.6 35.8 %shard_map.77 = (f32[12,96,256]{2,1,0:T(8,128)S(1)}, f32[12,96,256]{2,1,0:T(8,128)S(1)}, f32[12,96,256]{2,1,0:T(8,128)S(1)}, f32[12,96,256]{2,1,0:T(8,128)S(1)},...) custom-call(f32[12]{0:T(128)} %scale_hbm.1, f32[12,96,256]{2,1,0:T(8,128)} %forcing_ref.1, f32[96,256]{1,0:T(8,128)} %metric_ref.1, ...), custom_call_target="tpu_custom_call" | custom-call | tf_op jit(solution)/shard_map/pallas_call | solution.py:687
  36.5 1.8 %shard_map.78 = (f32[12,96,256]{2,1,0:T(8,128)}, f32[12,96,256]{2,1,0:T(8,128)}) custom-call(f32[12,96,256]{2,1,0:T(8,128)S(1)} %get-tuple-element.8.r0, f32[12,96,256]{2,1,0:T(8,128)S(1)} %get-tuple-element.9.r1, f32[12,96,256]{2,1,0:T(8,128)S(1)} %get-tuple-element.10.r2, f32[12,96,256]{2,1,0:T(8,128)S(1)} %get-tuple-element.11.u2, ...), custom_call_target="tpu_custom_call" | custom-call | tf_op jit(solution)/shard_map/pallas_call | solution.py:726

commit v10 on v9

--- a/solution.py
+++ b/solution.py
@@ -411,8 +411,8 @@
             + jnp.dot(zcat[g, lo:hi, :cols], table_ref[2 * cols:, :],
                       preferred_element_type=f32))
 
-    cut = (per + 1) // 2
-    parts_of = [(0, cut), (cut, per)]
+    third_of = per // 3
+    parts_of = [(0, third_of), (third_of, 2 * third_of), (2 * third_of, per)]
 
     def over(part, body, carry=0):
         return lax.fori_loop(part[0], part[1], body, carry, unroll=UNROLL)
@@ -532,21 +532,26 @@
                         line, axis=0, keepdims=True)
                 return carry
 
-            one, two = parts_of
+            one, two, three = parts_of
             over(one, first)
             multiply(g, grad_ref, one)
             over(two, first)
             over(one, second)
             multiply(g, grad_ref, two)
+            over(three, first)
+            over(two, second)
+            multiply(g, grad_ref, three)
             if it < ITERS - 1:
                 third = finish(g, it, base)
                 multiply(g, div_ref, one)
-                over(two, second)
+                over(three, second)
                 tops = over(one, third, (zero, zero))
                 multiply(g, div_ref, two)
-                send(k + groups, over(two, third, tops))
+                tops = over(two, third, tops)
+                multiply(g, div_ref, three)
+                send(k + groups, over(three, third, tops))
             else:
-                over(two, second)
+                over(three, second)
 
     high = lax.broadcasted_iota(jnp.int32, (FIELD, LANES), 0)
     wide = lax.broadcasted_iota(jnp.int32, (FIELD, LANES), 1)
@@ -572,10 +577,8 @@
     share(0, line, near_tx, near_rx, near)
     for g in range(groups):
         third = finish(g, ITERS - 1, g * per)
-        multiply(g, div_ref, one)
-        tops = over(one, third, (zero, zero))
-        multiply(g, div_ref, two)
-        send(ITERS * groups + g, over(two, third, tops))
+        multiply(g, div_ref, (0, per))
+        send(ITERS * groups + g, over((0, per), third, (zero, zero)))
     share(1, gather(0, near_rx), far_tx, far_rx, far)
     for g in range(groups):
         k = ITERS * groups + g

time: 38.4 us -> 38.1 us (level)
  Pallas kernels: 37.7 us -> 37.3 us
where the time goes in v10:
time: 38.1 us; the launch traced here: 38 us
  Pallas kernels  37.3 us (98%)
  between operations  0.64 us (2%)
    pallas_call x1, Pallas kernels, shards(): pl.pallas_call(functools.partial(kernel, nc, ns, modes, groups), out_shap...  35.5 us
    pallas_call x1, Pallas kernels, shards(): pl.pallas_call(node_order, out_shape=[shape] * 2, in_specs=[vm] * 6, out_...  1.82 us

profile of v10, /device:TPU:1, one launch (start us, length us, event | category | flops | bytes accessed | tf_op | source)
XLA Modules:
  0.0 38.0 jit_solution(12164445601794286266)
XLA Ops:
  0.6 35.5 %shard_map.77 = (f32[12,96,256]{2,1,0:T(8,128)S(1)}, f32[12,96,256]{2,1,0:T(8,128)S(1)}, f32[12,96,256]{2,1,0:T(8,128)S(1)}, f32[12,96,256]{2,1,0:T(8,128)S(1)},...) custom-call(f32[12]{0:T(128)} %scale_hbm.1, f32[12,96,256]{2,1,0:T(8,128)} %forcing_ref.1, f32[96,256]{1,0:T(8,128)} %metric_ref.1, ...), custom_call_target="tpu_custom_call" | custom-call | tf_op jit(solution)/shard_map/pallas_call | solution.py:690
  36.1 1.8 %shard_map.78 = (f32[12,96,256]{2,1,0:T(8,128)}, f32[12,96,256]{2,1,0:T(8,128)}) custom-call(f32[12,96,256]{2,1,0:T(8,128)S(1)} %get-tuple-element.8.r0, f32[12,96,256]{2,1,0:T(8,128)S(1)} %get-tuple-element.9.r1, f32[12,96,256]{2,1,0:T(8,128)S(1)} %get-tuple-element.10.r2, f32[12,96,256]{2,1,0:T(8,128)S(1)} %get-tuple-element.11.u2, ...), custom_call_target="tpu_custom_call" | custom-call | tf_op jit(solution)/shard_map/pallas_call | solution.py:729
